TPU v7x, 256 devices: a 8x8x2 block of a 8x8x16 slice. The times are simulated.
256 devices in a mesh: groups: 2 (over z), adapter: 16 (over x, core), tensor: 8 (over y).
Axes of the slice: x: 8, y: 8, z: 2, core: 2. Of those that a mesh axis runs over, the one named last changes fastest.
The devices are a block of a 8x8x16 slice.
Arguments:
- tokens: bfloat16 [8192, 8192], P(('groups', 'adapter'), 'tensor'), parts along dimension 0, may hold values from -6 to 6
- query_weight: bfloat16 [8192, 8192], P('tensor', 'adapter'), may hold values from -0.0625 to 0.0625
- adapter_down_weight: bfloat16 [512, 16, 8192], P('adapter', None, 'tensor'), may hold values from -0.0625 to 0.0625
- adapter_up_weight: bfloat16 [512, 16, 8192], P('adapter'), may hold values from -1.5 to 1.5
- block_adapter_ids: int32 [64], P('groups'), parts along dimension 0, may hold values from 0 to 511, as said below
- block_live_count: int32 [64], P('groups'), parts along dimension 0, may hold values from 1 to 128
- adapter_slot_index: int32 [1024], P('groups'), parts along dimension 0, may hold values from 0 to 511, as said below
Outputs:
- query: bfloat16 [8192, 8192], P(('groups', 'tensor'), 'adapter'), parts along dimension 0
There are 2 independent parts, one for each index of `groups`. A program takes and returns all parts, laid end to end along the dimension named above; an argument that names none is the same for every part. Nothing has to cross between parts.
Inputs may be any that keep to these rules, and one draw needn't show every extreme that they name: Counting blocks by the owner range adapter_slot_index[block_adapter_ids[k]] // 32, no owner has more than 4 blocks, and one owner has exactly 4 in every draw. `adapter_slot_index`: A permutation: each slot holds exactly one adapter.
All inputs are finite; a program needn't handle non-finite values.
Results may differ from a plain program's by a relative error of at most 0.014.
Values may be sent and summed in bfloat16 or wider, within the bound.
No kernel may reach another device: no remote copies, remote signals or barrier semaphores. Data moves between devices by JAX's collectives and lax.ppermute only.
A program may use at most 128 MiB of HBM per device.

v0:
```python
import jax
import jax.numpy as jnp
from jax import lax
from jax.sharding import PartitionSpec as P

BLOCK = 128


adapter_scale = 2.0


def block_plan(block_adapter_ids, adapter_slot_index, owners, adapters_per_device, capacity):
    adapters = adapter_slot_index.shape[0]
    picked = block_adapter_ids[:, None] == jnp.arange(adapters, dtype=jnp.int32)[None, :]
    block_slot_index = jnp.sum(jnp.where(picked, adapter_slot_index[None, :], 0), axis=1)
    owner_of = block_slot_index // adapters_per_device
    local_slot = block_slot_index % adapters_per_device
    hit_table = (owner_of[:, None] == jnp.arange(owners, dtype=jnp.int32)[None, :]).astype(
        jnp.int32
    )
    before = jnp.cumsum(hit_table, axis=0) - hit_table
    order_in = jnp.sum(before * hit_table, axis=1)
    return (owner_of, local_slot, order_in, owner_of * capacity + order_in)


def on_device(
    tokens,
    query_weight,
    adapter_down_weight,
    adapter_up_weight,
    block_adapter_ids,
    block_live_count,
    adapter_slot_index,
):
    owners = lax.axis_size("adapter")
    my_index = lax.axis_index("adapter")
    tok_dev = tokens.shape[0]
    features = tokens.shape[1]
    adapters_per_device = adapter_down_weight.shape[0]
    rank_width = adapter_down_weight.shape[1]
    blocks = block_adapter_ids.shape[0]
    blk_dev = blocks // owners
    capacity = 2 * blk_dev
    token_row_count = tok_dev * owners
    output_columns = query_weight.shape[1]
    owner_of, local_slot, order_in, packed = block_plan(
        block_adapter_ids, adapter_slot_index, owners, adapters_per_device, capacity
    )
    seat_ids = jnp.arange(capacity, dtype=jnp.int32)
    matches = (owner_of[None, :] == my_index) & (order_in[None, :] == seat_ids[:, None])
    filled = jnp.any(matches, axis=1)
    match_int = matches.astype(jnp.int32)
    local_adapter_rows = jnp.sum(match_int * local_slot[None, :], axis=1)
    token_keep_mask = filled.astype(jnp.bfloat16)
    positions = jnp.arange(BLOCK, dtype=jnp.int32)
    up_weight_packed = (
        jnp.take(adapter_up_weight, local_adapter_rows, axis=0) * token_keep_mask[:, None, None]
    )
    up_recv = lax.all_to_all(up_weight_packed, "adapter", split_axis=2, concat_axis=0, tiled=True)
    down_weight_packed = (
        jnp.take(adapter_down_weight, local_adapter_rows, axis=0) * token_keep_mask[:, None, None]
    )
    down_all = lax.all_gather(down_weight_packed, "adapter", axis=0, tiled=True)
    own_packed = lax.dynamic_slice_in_dim(packed, my_index * blk_dev, blk_dev)
    own_live = lax.dynamic_slice_in_dim(block_live_count, my_index * blk_dev, blk_dev)
    down_own = jnp.take(down_all, own_packed, axis=0)
    live_own = (positions[None, :] < own_live[:, None]).astype(jnp.float32)
    shrunk_own = jnp.einsum(
        "ksd,krd->ksr",
        tokens.reshape(blk_dev, BLOCK, features),
        down_own,
        preferred_element_type=jnp.float32,
    )
    shrunk_own = (
        (shrunk_own * live_own[:, :, None]).astype(jnp.bfloat16).reshape(tok_dev, rank_width)
    )
    token_piece = lax.all_gather(tokens, "adapter", axis=0, tiled=True)
    shrunk_piece = lax.all_gather(shrunk_own, "adapter", axis=0, tiled=True)
    query_product = jnp.dot(token_piece, query_weight, preferred_element_type=jnp.float32)
    up_weight_blocks = jnp.take(up_recv, packed, axis=0)
    adapter_output = jnp.einsum(
        "ksr,krf->ksf",
        shrunk_piece.reshape(blocks, BLOCK, rank_width),
        up_weight_blocks,
        preferred_element_type=jnp.float32,
    )
    partial_output = query_product + adapter_scale * adapter_output.reshape(
        token_row_count, output_columns
    )
    summed = lax.psum_scatter(
        partial_output.astype(jnp.bfloat16), "tensor", scatter_dimension=0, tiled=True
    )
    return summed


def solution(mesh):
    placed = (
        P(("groups", "adapter"), "tensor"),
        P("tensor", "adapter"),
        P("adapter", None, "tensor"),
        P("adapter", None, None),
        P("groups"),
        P("groups"),
        P("groups"),
    )
    return jax.shard_map(
        on_device,
        mesh=mesh,
        in_specs=placed,
        out_specs=P(("groups", "tensor"), "adapter"),
        check_vma=False,
    )
```

profile of v0, /device:TPU:513, one launch (start us, length us, event | category | flops | bytes accessed | tf_op | source)
XLA Modules:
  0.0 212.7 jit_solution(3576047556961893171)
XLA Ops:
  6.6 1.0 select_reduce_fusion
  7.7 0.2 select_reduce_fusion.1
  7.9 0.1 fusion.13
  8.0 0.1 select_reduce_fusion.2
  8.1 1.8 gather_fusion
  9.9 0.7 select_multiply_fusion.1
  10.8 0.7 all-gather.3.cloned.1.call-update
  11.6 4.0 %gather_fusion.2 = bf16[4,16,8192]{2,1,0:T(8,128)(2,1)S(1)} fusion(bf16[32,16,8192]{2,1,0:T(8,128)(2,1)} %param.10, s32[1024]{0:T(1024)S(1)} %pad_clamp_fusion.2), kind=kCustom, calls=%fused_computation.2 | custom fusion | bytes 2097168 | tf_op jit(solution)/shard_map/jit(_take)/gather | solution.py:57
  15.6 0.2 select_multiply_fusion
  15.7 8.3 %copy.23 = bf16[4,16,8192]{1,0,2:T(4,128)(2,1)} copy(bf16[4,16,8192]{2,1,0:T(8,128)(2,1)S(1)} %select_multiply_fusion) | data formatting | bytes 2097152 | tf_op jit(solution)/shard_map/mul | solution.py:57
  24.0 11.2 %reshape.207 = bf16[16,2,16384]{2,1,0:T(2,128)(2,1)} reshape(bf16[8192,4,16]{2,1,0:T(4,128)(2,1)} %bitcast.48) | data formatting | bytes 2097152
  35.3 23.9 %all-to-all-start = ((bf16[16,2,16384]{2,1,0:T(2,128)(2,1)}), bf16[16,2,16384]{2,1,0:T(2,128)(2,1)S(1)}, u32[]{:S(2)}, u32[]{:S(2)}) async-start(bf16[16,2,16384]{2,1,0:T(2,128)(2,1)} %reshape.207), calls=%async_computation | async-start | bytes 2097152 | tf_op jit(solution)/shard_map/all_to_all | solution.py:59
  59.3 0.1 compare_and_fusion.2
  59.5 27.7 %all-to-all-done = bf16[16,2,16384]{2,1,0:T(2,128)(2,1)S(1)} async-done(((bf16[16,2,16384]{2,1,0:T(2,128)(2,1)}), bf16[16,2,16384]{2,1,0:T(2,128)(2,1)S(1)}, u32[]{:S(2)}, u32[]{:S(2)}) %all-to-all-start) | async-done | bytes 1048608 | tf_op jit(solution)/shard_map/all_to_all | solution.py:59
  87.2 7.6 %reshape.208 = bf16[8192,4,16]{2,1,0:T(4,128)(2,1)} reshape(bf16[16,2,16384]{2,1,0:T(2,128)(2,1)S(1)} %all-to-all-done) | data formatting | bytes 2097152
  94.8 10.8 %copy.28 = bf16[4,16,16,512]{3,1,0,2:T(8,128)(2,1)S(1)} copy(bf16[4,16,16,512]{1,0,3,2:T(4,128)(2,1)} %bitcast.49) | data formatting | bytes 2097152 | tf_op jit(solution)/shard_map/all_to_all | solution.py:59
  105.6 0.6 gather_fusion.3
  106.2 2.2 %gather_fusion.1 = bf16[2,16,1024]{2,1,0:T(8,128)(2,1)S(1)} fusion(bf16[64,16,1024]{2,1,0:T(8,128)(2,1)} %all-gather.5.cloned.1.call-done, s32[1024]{0:T(1024)S(1)} %pad_clamp_fusion.1), kind=kCustom, calls=%fused_computation.1 | custom fusion | bytes 131080 | tf_op jit(solution)/shard_map/jit(_take)/gather | solution.py:66
  108.4 0.3 fusion.2
  108.7 17.2 %all_gather.11 = bf16[4096,16]{0,1:T(8,128)(2,1)S(1)} all-gather(bf16[256,16]{0,1:T(8,128)(2,1)S(1)} %bitcast.52), channel_id=1, replica_groups=mesh['groups'=2,'adapter'=16,'tensor'=8] {'adapter'}, dimensions={0}, use_global_device_ids=true | all-gather | bytes 139264 | tf_op jit(solution)/shard_map/all_gather | solution.py:78
  125.9 4.5 %broadcast_multiply_fusion = f32[32,128,512]{2,1,0:T(8,128)} fusion(bf16[32,16,512]{2,1,0:T(8,128)(2,1)S(1)} %gather_fusion.3, pred[32]{0:T(512)(128)(4,1)S(1)} %get-tuple-element.7, bf16[4096,16]{0,1:T(8,128)(2,1)S(1)} %all_gather.11), kind=kOutput, calls=%fused_computation.6 | convolution fusion | flops 69468160 | bytes 9044000 | tf_op jit(solution)/shard_map/ksr,krf->ksf/dot_general | solution.py:81
  130.4 9.4 %all-gather.3.cloned.1.call-done = bf16[4096,1024]{1,0:T(8,128)(2,1)} async-done(((bf16[256,1024]{1,0:T(8,128)(2,1)}), bf16[4096,1024]{1,0:T(8,128)(2,1)}) %all-gather.3.cloned.1.call-update) | async-done | bytes 8388624 | tf_op jit(solution)/shard_map/all_gather | solution.py:77
  139.8 10.7 %fusion = bf16[4096,512]{1,0:T(8,128)(2,1)} fusion(f32[32,128,512]{2,1,0:T(8,128)} %broadcast_multiply_fusion, bf16[4096,1024]{1,0:T(8,128)(2,1)} %all-gather.3.cloned.1.call-done, bf16[1024,512]{1,0:T(8,128)(2,1)S(1)} %copy-done), kind=kOutput, calls=%fused_computation.5 | convolution fusion | flops 4299161600 | bytes 22020096 | tf_op jit(solution)/shard_map/dot_general | solution.py:79
  150.6 55.6 %reduce-scatter.2.cloned.1.call-done = bf16[512,512]{1,0:T(8,128)(2,1)} async-done(((bf16[4096,512]{1,0:T(8,128)(2,1)}), bf16[512,512]{1,0:T(8,128)(2,1)}) %reduce-scatter.2.cloned.1.call-update) | async-done | bytes 524304 | tf_op jit(solution)/shard_map/reduce_scatter | solution.py:90
  (27 shorter events, 0.6 us)
Async XLA Ops:
  6.5 133.2 %copy-start = (bf16[1024,512]{1,0:T(8,128)(2,1)S(1)}, bf16[1024,512]{1,0:T(8,128)(2,1)}, u32[]{:S(2)}) copy-start(bf16[1024,512]{1,0:T(8,128)(2,1)} %param.8) | copy-start | bytes 3145732
  6.6 99.6 %all-gather.5.cloned.1.call-start = ((), (), s32[]{:S(2)}) async-start(), calls=%async_computation.3 | async-start | bytes 2228224 | tf_op jit(solution)/shard_map/all_gather | solution.py:63
  10.7 129.0 %all-gather.3.cloned.1.call-start = ((), (), s32[]{:S(2)}) async-start(), calls=%async_computation.2 | async-start | bytes 8912896 | tf_op jit(solution)/shard_map/all_gather | solution.py:77
  15.7 43.5 %copy-start.2 = (s32[32]{0:T(128)S(1)}, s32[32]{0:T(128)}, u32[]{:S(2)}) copy-start(s32[32]{0:T(128)} %param.12) | copy-start | bytes 388
  35.3 51.9 %all-to-all-start = ((bf16[16,2,16384]{2,1,0:T(2,128)(2,1)}), bf16[16,2,16384]{2,1,0:T(2,128)(2,1)S(1)}, u32[]{:S(2)}, u32[]{:S(2)}) async-start(bf16[16,2,16384]{2,1,0:T(2,128)(2,1)} %reshape.207), calls=%async_computation | async-start | bytes 2097152 | tf_op jit(solution)/shard_map/all_to_all | solution.py:59
  59.2 147.0 %reduce-scatter.2.cloned.1.call-start = ((), (), s32[]{:S(2)}) async-start(), calls=%async_computation.4 | async-start | bytes 4718592 | tf_op jit(solution)/shard_map/reduce_scatter | solution.py:90
  59.5 48.9 %copy-start.1 = (bf16[256,1024]{1,0:T(8,128)(2,1)S(1)}, bf16[256,1024]{1,0:T(8,128)(2,1)}, u32[]{:S(2)}) copy-start(bf16[256,1024]{1,0:T(8,128)(2,1)} %param.7) | copy-start | bytes 1572868
Sparse Core Ops, SparseCore 0:
  10.9 65.9 all-gather.4
  78.7 61.0 all-gather.2
  150.7 55.4 reduce-scatter.1
where the time goes:
time: 213 us
  waiting for transfers between devices  93.5 us (44%)
  local copies, waits for them, and re-layouts  46.6 us (22%)
  starting transfers between devices  24 us (11%)
  blocking collectives  17.2 us (8%)
  matrix products  15.5 us (7%)
  between operations  13.3 us (6%)
  other arithmetic  2.65 us (1%)
    reduce_scatter x1, waiting for transfers between devices, on_device(): lax.psum_scatter(partial_output.astype(jnp.bfloat16), 'tensor', scatter_d...  55.6 us
    all_to_all x1, waiting for transfers between devices, on_device(): lax.all_to_all(up_weight_packed, 'adapter', split_axis=2, concat_axis=0,...  27.7 us
    all_to_all x1, starting transfers between devices, on_device(): lax.all_to_all(up_weight_packed, 'adapter', split_axis=2, concat_axis=0,...  23.9 us
    unnamed x8, local copies, waits for them, and re-layouts  18.9 us
    all_gather x1, blocking collectives, on_device(): shrunk_piece = lax.all_gather(shrunk_own, 'adapter', axis=0, tiled=True)  17.2 us
    all_to_all x1, local copies, waits for them, and re-layouts, on_device(): lax.all_to_all(up_weight_packed, 'adapter', split_axis=2, concat_axis=0,...  10.8 us
    dot_general x1, matrix products, on_device(): jnp.dot(token_piece, query_weight, preferred_element_type=jnp.float32)  10.7 us
    all_gather x1, waiting for transfers between devices, on_device(): token_piece = lax.all_gather(tokens, 'adapter', axis=0, tiled=True)  9.36 us
  transfers between devices with their start and end apart: 4, of which 3 were waited for; matrix products, arithmetic and copies ran while one was open for 23% of the time, Pallas kernels for 0%

commit v1 on v0

v1 whole, which is shorter than its diff:
```python
import functools

import jax
import jax.numpy as jnp
from jax import lax
from jax.experimental import pallas as pl
from jax.experimental.pallas import tpu as pltpu
from jax.sharding import PartitionSpec as P


BLOCK = 128
CORES = 2
CHUNKS = 1

adapter_scale = 2.0


bf16 = jnp.bfloat16
f32 = jnp.float32
i32 = jnp.int32
VMEM = pl.BlockSpec(memory_space=pltpu.VMEM)
SMEM = pl.BlockSpec(memory_space=pltpu.SMEM)
ANY = pl.BlockSpec(memory_space=pl.ANY)


def shift_chips(v, chips, step):
    pairs = [
        (x * CORES + c, ((x + step) % chips) * CORES + c)
        for x in range(chips)
        for c in range(CORES)
    ]
    return lax.ppermute(v, "adapter", pairs)


def swap_cores(v, chips):
    return lax.ppermute(v, "adapter", [(i, i ^ 1) for i in range(chips * CORES)])


def shift_slices(v, slices, step):
    return lax.ppermute(v, "tensor", [(y, (y + step) % slices) for y in range(slices)])


def shift_slices_swap(v, adapters, slices, step):
    pairs = [
        (a * slices + y, (a ^ 1) * slices + (y + step) % slices)
        for a in range(adapters)
        for y in range(slices)
    ]
    return lax.ppermute(v, ("adapter", "tensor"), pairs)


def plan_kernel(
    owners, slices, seats, where, ids, live, index, down, up,
    table, down_out, up_out, counts, seat_slot, sems
):
    slots = down.shape[0]
    rank = down.shape[1]
    blocks = ids.shape[0]
    a, y = where[0], where[1]
    c = lax.rem(a, CORES)
    for i in range(owners):
        counts[i] = 0
    for s in range(seats):
        seat_slot[s] = 0

    def block(k, _):
        slot = index[ids[k]]
        owner = lax.div(slot, slots)
        local = slot - owner * slots
        seat = jnp.minimum(counts[owner], seats - 1)
        counts[owner] = seat + 1
        table[0, k] = owner
        table[1, k] = seat
        table[2, k] = jnp.where(
            owner == a, seat, jnp.where(lax.div(owner, CORES) == lax.div(a, CORES), seats + seat, -1)
        )
        table[3, k] = live[k]

        @pl.when(owner == a)
        def _():
            seat_slot[seat] = local

        return 0

    lax.fori_loop(0, blocks, block, 0)
    cols = up.shape[2] // owners
    parts = slices // seats
    part = cols // parts
    copies = []
    for s in range(seats):
        copies.append(
            pltpu.make_async_copy(
                down.at[seat_slot[s]], down_out.at[pl.ds(s * rank, rank)], sems.at[s]
            )
        )
    up_slot = seat_slot[lax.div(y, parts)]
    low = lax.rem(y, parts) * part
    for d in range(owners):
        copies.append(
            pltpu.make_async_copy(
                up.at[up_slot, :, pl.ds(pl.multiple_of(d * cols + low, part), part)],
                up_out.at[d],
                sems.at[seats + d],
            )
        )
    for copy in copies:
        copy.start()
    for copy in copies:
        copy.wait()


def pick_kernel(rank, blk_dev, table, c_ref, shr, out):
    chips, _, _ = shr.shape
    lane = lax.broadcasted_iota(i32, (rank, BLOCK), 1)
    c = c_ref[0]
    for src in range(chips):
        for j in range(blk_dev):
            k = (src * CORES + c) * blk_dev + j
            seat = table[2, k]
            at = pl.multiple_of(jnp.maximum(seat, 0) * rank, rank)
            v = shr[src, pl.ds(at, rank), j * BLOCK : (j + 1) * BLOCK]
            live = jnp.where(seat < 0, 0, table[3, k])
            v = jnp.where(lane < live, v.astype(f32), 0.0)
            out[src, :, j * BLOCK : (j + 1) * BLOCK] = v.astype(bf16)


def extra_kernel(blk_dev, table, shr, up, y_ref, out):
    owners, rank, rows = shr.shape
    _, blk_chip, _, part = up.shape
    cols = out.shape[1]
    parts = cols // part
    y = y_ref[0]
    total = [jnp.zeros((rank, rows), f32) for _ in range(CORES)]
    for o in range(owners):
        total[o % CORES] = total[o % CORES] + shr[o].astype(f32)
    for b in range(blk_chip):
        j = b % blk_dev
        s = total[b // blk_dev][:, j * BLOCK : (j + 1) * BLOCK].astype(bf16)
        seat = table[1, y * blk_chip + b]
        for h in range(parts):
            u = up[seat * parts + h, b]
            e = lax.dot_general(s, u, (((0,), (0,)), ((), ())), preferred_element_type=f32)
            out[b * BLOCK : (b + 1) * BLOCK, h * part : (h + 1) * part] = adapter_scale * e


def finish_kernel(chunks, *refs):
    c_ref, extra = refs[0], refs[1]
    out = refs[-1]
    n = refs[2].shape[0]
    rows = n * chunks
    c = c_ref[0]
    for q in range(chunks):
        own, dn_own, up_own, oth, dn_oth, up_oth = refs[2 + 6 * q : 8 + 6 * q]
        at = pl.multiple_of(c * rows + q * n, n)
        v = own[...].astype(f32) + dn_own[...].astype(f32) + up_own[...].astype(f32)
        out[pl.ds(at, n)] = (v + extra[pl.ds(at, n)]).astype(bf16)
        at = pl.multiple_of((1 - c) * rows + q * n, n)
        v = oth[...].astype(f32) + dn_oth[...].astype(f32) + up_oth[...].astype(f32)
        out[pl.ds(at, n)] = (v + extra[pl.ds(at, n)]).astype(bf16)


def on_device(
    tokens,
    query_weight,
    adapter_down_weight,
    adapter_up_weight,
    block_adapter_ids,
    block_live_count,
    adapter_slot_index,
):
    owners = lax.axis_size("adapter")
    slices = lax.axis_size("tensor")
    chips = owners // CORES
    half = chips // 2
    a = lax.axis_index("adapter")
    y = lax.axis_index("tensor")
    x, c = a // CORES, a % CORES
    rows, feats = tokens.shape
    cols = query_weight.shape[1]
    _, rank, _ = adapter_up_weight.shape
    blocks = block_adapter_ids.shape[0]
    seats = 2 * blocks // owners
    blk_dev = blocks // owners
    blk_chip = blk_dev * CORES
    parts = slices // seats
    part = cols // parts
    n = rows // CHUNKS

    chunks = [tokens[q * n : (q + 1) * n] for q in range(CHUNKS)]
    ups, dns = [], []
    for q in range(CHUNKS):
        ups.append([shift_chips(chunks[q], chips, 1)])
        dns.append([shift_chips(chunks[q], chips, -1)])
    w_oth = swap_cores(query_weight, chips)
    w_both = jnp.concatenate([query_weight, w_oth], axis=1)

    table, down_own, up_part = pl.pallas_call(
        functools.partial(plan_kernel, owners, slices, seats),
        out_shape=(
            jax.ShapeDtypeStruct((4, blocks), i32),
            jax.ShapeDtypeStruct((seats * rank, feats), bf16),
            jax.ShapeDtypeStruct((owners, rank, part), bf16),
        ),
        in_specs=[SMEM] * 4 + [ANY] * 2,
        out_specs=(SMEM, VMEM, VMEM),
        scratch_shapes=[
            pltpu.SMEM((owners,), i32),
            pltpu.SMEM((seats,), i32),
            pltpu.SemaphoreType.DMA((seats + owners,)),
        ],
        cost_estimate=pl.CostEstimate(flops=10**7, bytes_accessed=10**6, transcendentals=0),
    )(
        jnp.stack([a, y]),
        block_adapter_ids,
        block_live_count,
        adapter_slot_index,
        adapter_down_weight,
        adapter_up_weight,
    )
    down_oth = swap_cores(down_own, chips)
    down_chip = jnp.concatenate([down_own, down_oth], axis=0)
    up_part = lax.all_to_all(up_part, "adapter", 0, 0, tiled=True)
    up_all = jnp.take(up_part, table[0], axis=0)
    up_all = lax.all_to_all(
        up_all.reshape(slices, blk_chip, rank, part), "tensor", 0, 0, tiled=True
    )

    shr_buf = jnp.zeros((chips, CORES * seats * rank, rows), bf16)
    bufs = []

    def put(q, tok, d):
        nonlocal shr_buf
        src = (x + d) % chips
        p = jnp.dot(tok, w_both, preferred_element_type=f32).astype(bf16)
        bufs[q] = lax.dynamic_update_slice(bufs[q], p[None], (src, 0, 0))
        s = lax.dot_general(
            down_chip, tok, (((1,), (1,)), ((), ())), preferred_element_type=f32
        ).astype(bf16)
        shr_buf = lax.dynamic_update_slice(shr_buf, s[None], (src, 0, q * n))

    for q in range(CHUNKS):
        bufs.append(jnp.zeros((chips, n, CORES * cols), bf16))
        put(q, chunks[q], 0)
    for h in range(1, half + 1):
        for q in range(CHUNKS):
            if h == half:
                tok = jnp.concatenate([ups[q][-1], dns[q][-1]], axis=0)
                put(q, tok, half)
                continue
            put(q, ups[q][-1], -h)
            put(q, dns[q][-1], h)
            up, dn = ups[q][-1], dns[q][-1]
            if h == half - 1:
                up, dn = up[: n // 2], dn[n // 2 :]
            ups[q].append(shift_chips(up, chips, 1))
            dns[q].append(shift_chips(dn, chips, -1))

    shr = pl.pallas_call(
        functools.partial(pick_kernel, rank, blk_dev),
        out_shape=jax.ShapeDtypeStruct((chips, rank, rows), bf16),
        in_specs=[SMEM, SMEM, VMEM],
        out_specs=VMEM,
        cost_estimate=pl.CostEstimate(flops=10**7, bytes_accessed=10**6, transcendentals=0),
    )(table, c[None], shr_buf)
    shr, up_all = lax.optimization_barrier((shr, up_all))
    shr = lax.all_to_all(shr, "tensor", 0, 0, tiled=True)
    shr = jnp.sum(shr.astype(f32), axis=0).astype(bf16)
    shr = jnp.broadcast_to(shr[None], (owners, rank, rows))
    shr = lax.all_to_all(shr, "adapter", 0, 0, tiled=True)
    extra = pl.pallas_call(
        functools.partial(extra_kernel, blk_dev),
        out_shape=jax.ShapeDtypeStruct((blk_chip * BLOCK, cols), f32),
        in_specs=[SMEM, VMEM, VMEM, SMEM],
        out_specs=VMEM,
        cost_estimate=pl.CostEstimate(flops=10**7, bytes_accessed=10**6, transcendentals=0),
    )(table, shr, up_all, y[None])

    def mine(q, t):
        return lax.dynamic_index_in_dim(bufs[q], t % slices, 0, keepdims=False)

    m = n // 2
    dn, up = [], []
    for q in range(CHUNKS):
        far = mine(q, y + half)
        dn.append(shift_slices(far[:m], slices, -1))
        up.append(shift_slices(far[m:], slices, 1))
    ends = []
    for h in range(half - 1, 0, -1):
        for q in range(CHUNKS):
            d = mine(q, y + slices - h).astype(f32)
            u = mine(q, y + h).astype(f32)
            if h == half - 1:
                d = jnp.concatenate([d[:m] + dn[q].astype(f32), d[m:]], axis=0)
                u = jnp.concatenate([u[:m], u[m:] + up[q].astype(f32)], axis=0)
            else:
                d = d + dn[q].astype(f32)
                u = u + up[q].astype(f32)
            d, u = d.astype(bf16), u.astype(bf16)
            if h > 1:
                dn[q] = shift_slices(d, slices, -1)
                up[q] = shift_slices(u, slices, 1)
            else:
                last = mine(q, y)
                oth = swap_cores(last[:, cols:], chips)
                ends += [
                    last[:, :cols],
                    shift_slices(d[:, :cols], slices, -1),
                    shift_slices(u[:, :cols], slices, 1),
                    oth,
                    shift_slices_swap(d[:, cols:], owners, slices, -1),
                    shift_slices_swap(u[:, cols:], owners, slices, 1),
                ]
    return pl.pallas_call(
        functools.partial(finish_kernel, CHUNKS),
        out_shape=jax.ShapeDtypeStruct((CORES * rows, cols), bf16),
        in_specs=[SMEM] + [VMEM] * (1 + 6 * CHUNKS),
        out_specs=VMEM,
        cost_estimate=pl.CostEstimate(flops=10**7, bytes_accessed=10**6, transcendentals=0),
    )(c[None], extra, *ends)


def solution(mesh):
    placed = (
        P(("groups", "adapter"), "tensor"),
        P("tensor", "adapter"),
        P("adapter", None, "tensor"),
        P("adapter", None, None),
        P("groups"),
        P("groups"),
        P("groups"),
    )
    return jax.shard_map(
        on_device,
        mesh=mesh,
        in_specs=placed,
        out_specs=P(("groups", "tensor"), "adapter"),
        check_vma=False,
    )
```

time: 213 us -> 148 us (0.69)
  waiting for transfers between devices: 93.5 us -> 39.2 us
  local copies, waits for them, and re-layouts: 46.6 us -> 9.87 us
  starting transfers between devices: 24 us -> 54.6 us
  between operations: 13.3 us -> 0.45 us
  Pallas kernels: 0 us -> 9.92 us
  blocking collectives: 17.2 us -> 14.7 us
    reduce_scatter x1 -> x0, waiting for transfers between devices: 55.6 us -> none  [on_device(): lax.psum_scatter(partial_output.astype(jnp.bfloat16), 'tensor', scatter_d...]
    ppermute x0 -> x21, starting transfers between devices: none -> 43.6 us  [the longest x3 24.1 us: swap_cores(): lax.ppermute(v, 'adapter', [(i, i ^ 1) for i in range(chips * CORES)])]
    ppermute x0 -> x21, waiting for transfers between devices: none -> 35.3 us  [the longest x8 20.3 us: shift_slices(): lax.ppermute(v, 'tensor', [(y, (y + step) % slices) for y in range(slices)])]
    all_to_all x1 -> x3, waiting for transfers between devices: 27.7 us -> 3.84 us  [the longest x1 3.12 us: on_device(): up_part = lax.all_to_all(up_part, 'adapter', 0, 0, tiled=True)]
    all_gather x1 -> x0, blocking collectives: 17.2 us -> none  [on_device(): shrunk_piece = lax.all_gather(shrunk_own, 'adapter', axis=0, tiled=True)]
    all_to_all x0 -> x1, blocking collectives: none -> 14.7 us  [on_device(): shr = lax.all_to_all(shr, 'adapter', 0, 0, tiled=True)]
    unnamed x8 -> x23, local copies, waits for them, and re-layouts: 18.9 us -> 4.87 us
    all_to_all x1 -> x3, starting transfers between devices: 23.9 us -> 11 us  [the longest x1 3.79 us: on_device(): up_part = lax.all_to_all(up_part, 'adapter', 0, 0, tiled=True)]
  transfers between devices with their start and end apart: 4 -> 24, of which waited for: 3 -> 12; matrix products, arithmetic and copies ran while one was open for 23% -> 17% of each run, Pallas kernels for 0% -> 5%
where the time goes in v1:
time: 148 us; the launch traced here: 147 us
  starting transfers between devices  54.6 us (37%)
  waiting for transfers between devices  39.2 us (26%)
  blocking collectives  14.7 us (10%)
  matrix products  14.4 us (10%)
  Pallas kernels  9.92 us (7%)
  local copies, waits for them, and re-layouts  9.87 us (7%)
  other arithmetic  4.27 us (3%)
    ppermute x3, starting transfers between devices, swap_cores(): lax.ppermute(v, 'adapter', [(i, i ^ 1) for i in range(chips * CORES)])  24.1 us
    ppermute x8, waiting for transfers between devices, shift_slices(): lax.ppermute(v, 'tensor', [(y, (y + step) % slices) for y in range(slices)])  20.3 us
    ppermute x8, waiting for transfers between devices, shift_chips(): return lax.ppermute(v, 'adapter', pairs)  15.1 us
    all_to_all x1, blocking collectives, on_device(): shr = lax.all_to_all(shr, 'adapter', 0, 0, tiled=True)  14.7 us
    ppermute x8, starting transfers between devices, shift_chips(): return lax.ppermute(v, 'adapter', pairs)  9.82 us
    dot_general x8, matrix products, put(): p = jnp.dot(tok, w_both, preferred_element_type=f32).astype(bf16)  8.81 us
    ppermute x8, starting transfers between devices, shift_slices(): lax.ppermute(v, 'tensor', [(y, (y + step) % slices) for y in range(slices)])  8.16 us
    dot_general x8, matrix products, put(): lax.dot_general(down_chip, tok, (((1,), (1,)), ((), ())), preferred_eleme...  5.61 us
  transfers between devices with their start and end apart: 24, of which 12 were waited for; matrix products, arithmetic and copies ran while one was open for 17% of the time, Pallas kernels for 5%

profile of v1, /device:TPU:513, one launch (start us, length us, event | category | flops | bytes accessed | tf_op | source)
XLA Modules:
  0.0 147.4 jit_solution(235372887100496698)
XLA Ops:
  0.0 2.2 %collective-permute-start.1 = (bf16[256,1024]{1,0:T(8,128)(2,1)}, bf16[256,1024]{1,0:T(8,128)(2,1)S(1)}, u32[]{:S(2)}, u32[]{:S(2)}) collective-permute-start(bf16[256,1024]{1,0:T(8,128)(2,1)} %param.7), channel_id=1, source_target_pairs={{0,16},{8,24},{16,32},{24,40},{32,48},{40,56},{48,64},{56,72},{64,... | collective-permute-start | bytes 1572872 | tf_op jit(solution)/shard_map/ppermute | solution.py:32
  2.2 2.2 %collective-permute-start.2 = (bf16[256,1024]{1,0:T(8,128)(2,1)}, bf16[256,1024]{1,0:T(8,128)(2,1)}, u32[]{:S(2)}, u32[]{:S(2)}) collective-permute-start(bf16[256,1024]{1,0:T(8,128)(2,1)} %param.7), channel_id=1, source_target_pairs={{0,112},{8,120},{16,0},{24,8},{32,16},{40,24},{48,32},{56,40},{64,... | collective-permute-start | bytes 1572872 | tf_op jit(solution)/shard_map/ppermute | solution.py:32
  4.4 19.3 %collective-permute-start.9 = (bf16[1024,512]{1,0:T(8,128)(2,1)}, bf16[1024,512]{1,0:T(8,128)(2,1)S(1)}, u32[]{:S(2)}, u32[]{:S(2)}) collective-permute-start(bf16[1024,512]{1,0:T(8,128)(2,1)} %param.8), channel_id=1, source_target_pairs={{0,8},{8,0},{16,24},{24,16},{32,40},{40,32},{48,56},{56,48},{64,72... | collective-permute-start | bytes 3145736 | tf_op jit(solution)/shard_map/ppermute | solution.py:36
  24.3 3.2 %shard_map.73 = (s32[4,32]{1,0:T(4,128)}, bf16[64,1024]{1,0:T(8,128)(2,1)}, bf16[16,16,256]{2,1,0:T(8,128)(2,1)}) custom-call(s32[2]{0:T(128)} %pad_add_fusion.where, s32[32]{0:T(128)} %ids.1, s32[32]{0:T(128)} %live.1, s32[512]{0:T(512)} %index.1, bf16[32,16,1024]{2,1,0:T(8,128)(2,1)} %down.1, bf16[32,16,8192]{2,1,0:T(8,128)(2,1)} %up.1), custom_call_target="tpu_custom_call" | custom-call | flops 10000000 | bytes 1000000 | tf_op jit(solution)/shard_map/pallas_call | solution.py:197
  27.7 3.8 %all-to-all-start = ((bf16[16,16,256]{2,1,0:T(8,128)(2,1)}), bf16[16,16,256]{2,1,0:T(8,128)(2,1)S(1)}, u32[]{:S(2)}, u32[]{:S(2)}) async-start(bf16[16,16,256]{2,1,0:T(8,128)(2,1)} %get-tuple-element.12), calls=%async_computation | async-start | bytes 262144 | tf_op jit(solution)/shard_map/all_to_all | solution.py:222
  37.7 3.1 %all-to-all-done = bf16[16,16,256]{2,1,0:T(8,128)(2,1)S(1)} async-done(((bf16[16,16,256]{2,1,0:T(8,128)(2,1)}), bf16[16,16,256]{2,1,0:T(8,128)(2,1)S(1)}, u32[]{:S(2)}, u32[]{:S(2)}) %all-to-all-start) | async-done | bytes 131104 | tf_op jit(solution)/shard_map/all_to_all | solution.py:222
  42.4 3.6 %all-to-all-start.1 = ((bf16[8,4,16,256]{3,2,1,0:T(8,128)(2,1)}), bf16[8,4,16,256]{3,2,1,0:T(8,128)(2,1)S(1)}, u32[]{:S(2)}, u32[]{:S(2)}) async-start(bf16[8,4,16,256]{3,2,1,0:T(8,128)(2,1)} %broadcast_select_fusion), calls=%async_computation.1 | async-start | bytes 524288 | tf_op jit(solution)/shard_map/all_to_all | solution.py:224
  46.0 3.9 %collective-permute-done.3 = bf16[256,1024]{1,0:T(8,128)(2,1)} collective-permute-done((bf16[256,1024]{1,0:T(8,128)(2,1)S(1)}, bf16[256,1024]{1,0:T(8,128)(2,1)}, u32[]{:S(2)}, u32[]{:S(2)}) %collective-permute-start.3) | collective-permute-done | bytes 524320 | tf_op jit(solution)/shard_map/ppermute | solution.py:32
  53.4 2.3 %collective-permute-done.4 = bf16[256,1024]{1,0:T(8,128)(2,1)} collective-permute-done((bf16[256,1024]{1,0:T(8,128)(2,1)}, bf16[256,1024]{1,0:T(8,128)(2,1)}, u32[]{:S(2)}, u32[]{:S(2)}) %collective-permute-start.4) | collective-permute-done | bytes 524320 | tf_op jit(solution)/shard_map/ppermute | solution.py:32
  57.7 1.8 %fusion.7 = bf16[8,256,1024]{2,1,0:T(8,128)(2,1)S(1)} fusion(bf16[8,256,1024]{2,1,0:T(8,128)(2,1)S(1)} %fusion.5, s32[]{:T(128)S(6)} %select_n.161, bf16[256,1024]{1,0:T(8,128)(2,1)} %collective-permute-done.2, bf16[1024,1024]{1,0:T(8,128)(2,1)S(1)} %copy-done.4), kind=kOutput, calls=%fused_computation.16 | convolution fusion | flops 537133056 | bytes 3145732 | tf_op jit(solution)/shard_map/dot_general | solution.py:234
  59.4 1.8 %fusion.9 = bf16[8,256,1024]{2,1,0:T(8,128)(2,1)S(1)} fusion(bf16[8,256,1024]{2,1,0:T(8,128)(2,1)S(1)} %fusion.7, s32[]{:T(128)S(6)} %select_n.163, bf16[256,1024]{1,0:T(8,128)(2,1)} %collective-permute-done.3, bf16[1024,1024]{1,0:T(8,128)(2,1)S(1)} %copy-done.4), kind=kOutput, calls=%fused_computation.18 | convolution fusion | flops 537133056 | bytes 3145732 | tf_op jit(solution)/shard_map/dot_general | solution.py:234
  61.2 1.8 %fusion.11 = bf16[8,256,1024]{2,1,0:T(8,128)(2,1)S(1)} fusion(bf16[8,256,1024]{2,1,0:T(8,128)(2,1)S(1)} %fusion.9, s32[]{:T(128)S(6)} %select_n.165, bf16[256,1024]{1,0:T(8,128)(2,1)} %collective-permute-done.4, bf16[1024,1024]{1,0:T(8,128)(2,1)S(1)} %copy-done.4), kind=kOutput, calls=%fused_computation.20 | convolution fusion | flops 537133056 | bytes 3145732 | tf_op jit(solution)/shard_map/dot_general | solution.py:234
  63.8 5.2 %collective-permute-done.6 = bf16[256,1024]{1,0:T(8,128)(2,1)S(1)} collective-permute-done((bf16[256,1024]{1,0:T(8,128)(2,1)}, bf16[256,1024]{1,0:T(8,128)(2,1)S(1)}, u32[]{:S(2)}, u32[]{:S(2)}) %collective-permute-start.6) | collective-permute-done | bytes 524320 | tf_op jit(solution)/shard_map/ppermute | solution.py:32
  69.0 2.5 %collective-permute-start.8 = (bf16[128,1024]{1,0:T(8,128)(2,1)S(1)}, bf16[128,1024]{1,0:T(8,128)(2,1)S(1)}, u32[]{:S(2)}, u32[]{:S(2)}) collective-permute-start(bf16[128,1024]{1,0:T(8,128)(2,1)S(1)} %slice.99), channel_id=1, source_target_pairs={{0,112},{8,120},{16,0},{24,8},{32,16},{40,24},{48,32},{56,40},{64,... | collective-permute-start | bytes 786440 | tf_op jit(solution)/shard_map/ppermute | solution.py:32
  73.0 2.9 %collective-permute-done.8 = bf16[128,1024]{1,0:T(8,128)(2,1)S(1)} collective-permute-done((bf16[128,1024]{1,0:T(8,128)(2,1)S(1)}, bf16[128,1024]{1,0:T(8,128)(2,1)S(1)}, u32[]{:S(2)}, u32[]{:S(2)}) %collective-permute-start.8) | collective-permute-done | bytes 262176 | tf_op jit(solution)/shard_map/ppermute | solution.py:32
  80.0 2.6 %collective-permute-done.10 = bf16[128,1024]{1,0:T(8,128)(2,1)S(1)} collective-permute-done((bf16[128,1024]{1,0:T(8,128)(2,1)S(1)}, bf16[128,1024]{1,0:T(8,128)(2,1)S(1)}, u32[]{:S(2)}, u32[]{:S(2)}) %collective-permute-start.10) | collective-permute-done | bytes 262176 | tf_op jit(solution)/shard_map/ppermute | solution.py:40
  87.1 2.8 %collective-permute-start.11 = (bf16[256,1024]{1,0:T(8,128)(2,1)S(1)}, bf16[256,1024]{1,0:T(8,128)(2,1)S(1)}, u32[]{:S(2)}, u32[]{:S(2)}) collective-permute-start(bf16[256,1024]{1,0:T(8,128)(2,1)S(1)} %pad_maximum_fusion), channel_id=1, source_target_pairs={{0,7},{1,0},{2,1},{3,2},{4,3},{5,4},{6,5},{7,6},{8,15},{9,8},{10,9... | collective-permute-start | bytes 1572872 | tf_op jit(solution)/shard_map/ppermute | solution.py:40
  89.9 6.2 %collective-permute-done.15 = bf16[256,1024]{1,0:T(8,128)(2,1)S(1)} collective-permute-done((bf16[256,1024]{1,0:T(8,128)(2,1)S(1)}, bf16[256,1024]{1,0:T(8,128)(2,1)S(1)}, u32[]{:S(2)}, u32[]{:S(2)}) %collective-permute-start.15) | collective-permute-done | bytes 524320 | tf_op jit(solution)/shard_map/ppermute | solution.py:40
  97.9 9.3 %collective-permute-done.16 = bf16[256,1024]{1,0:T(8,128)(2,1)S(1)} collective-permute-done((bf16[256,1024]{1,0:T(8,128)(2,1)S(1)}, bf16[256,1024]{1,0:T(8,128)(2,1)S(1)}, u32[]{:S(2)}, u32[]{:S(2)}) %collective-permute-start.16) | collective-permute-done | bytes 524320 | tf_op jit(solution)/shard_map/ppermute | solution.py:40
  108.5 4.7 %collective-permute-start.18 = (bf16[256,512]{1,0:T(8,128)(2,1)S(1)}, bf16[256,512]{1,0:T(8,128)(2,1)}, u32[]{:S(2)}, u32[]{:S(2)}) collective-permute-start(bf16[256,512]{1,0:T(8,128)(2,1)S(1)} %get-tuple-element.27), channel_id=1, source_target_pairs={{0,8},{8,0},{16,24},{24,16},{32,40},{40,32},{48,56},{56,48},{64,72... | collective-permute-start | bytes 786440 | tf_op jit(solution)/shard_map/ppermute | solution.py:36
  116.1 3.6 %all-to-all-start.2 = ((bf16[8,16,256]{2,1,0:T(8,128)(2,1)}), bf16[8,16,256]{2,1,0:T(8,128)(2,1)S(1)}, u32[]{:S(2)}, u32[]{:S(2)}) async-start(bf16[8,16,256]{2,1,0:T(8,128)(2,1)} %shard_map.74), calls=%async_computation.2 | async-start | bytes 131072 | tf_op jit(solution)/shard_map/all_to_all | solution.py:266
  126.7 14.7 %all_to_all.20.shr = bf16[16,16,256]{2,1,0:T(8,128)(2,1)} all-to-all(bf16[16,16,256]{2,1,0:T(8,128)(2,1)S(1)} %broadcast_in_dim.87), channel_id=1, replica_groups=mesh['groups'=2,'adapter'=16,'tensor'=8] {'adapter'}, dimensions={0} | all-to-all | bytes 262144 | tf_op jit(solution)/shard_map/all_to_all | solution.py:269
  141.4 2.3 %shard_map.75.refs_1_ = f32[512,512]{1,0:T(8,128)} custom-call(s32[4,32]{1,0:T(4,128)} %get-tuple-element.10.table, bf16[16,16,256]{2,1,0:T(8,128)(2,1)} %all_to_all.20.shr, bf16[8,4,16,256]{3,2,1,0:T(8,128)(2,1)} %copy-done.3, s32[1]{0:T(128)} %bitcast.2.y_ref), custom_call_target="tpu_custom_call" | custom-call | flops 10000000 | bytes 1000000 | tf_op jit(solution)/shard_map/pallas_call | solution.py:270
  144.7 2.7 %shard_map.76 = bf16[512,512]{1,0:T(8,128)(2,1)} custom-call(s32[1]{0:T(128)} %bitcast.c_ref.refs_0_, f32[512,512]{1,0:T(8,128)} %shard_map.75.refs_1_, bf16[256,512]{1,0:T(8,128)(2,1)} %get-tuple-element.28.refs_2_, bf16[256,512]{1,0:T(8,128)(2,1)} %copy-done.8, bf16[256,512]{1,0:T(8,128)(2,1)} %copy-done.6, ...), custom_call_target="tpu_custom_call" | custom-call | flops 10000000 | bytes 1000000 | tf_op jit(solution)/shard_map/pallas_call | solution.py:313
  (96 shorter events, 38.7 us)
Async XLA Ops:
  0.0 35.0 %collective-permute-start.1 = (bf16[256,1024]{1,0:T(8,128)(2,1)}, bf16[256,1024]{1,0:T(8,128)(2,1)S(1)}, u32[]{:S(2)}, u32[]{:S(2)}) collective-permute-start(bf16[256,1024]{1,0:T(8,128)(2,1)} %param.7), channel_id=1, source_target_pairs={{0,16},{8,24},{16,32},{24,40},{32,48},{40,56},{48,64},{56,72},{64,... | collective-permute-start | bytes 1572872 | tf_op jit(solution)/shard_map/ppermute | solution.py:32
  2.2 39.2 %collective-permute-start.2 = (bf16[256,1024]{1,0:T(8,128)(2,1)}, bf16[256,1024]{1,0:T(8,128)(2,1)}, u32[]{:S(2)}, u32[]{:S(2)}) collective-permute-start(bf16[256,1024]{1,0:T(8,128)(2,1)} %param.7), channel_id=1, source_target_pairs={{0,112},{8,120},{16,0},{24,8},{32,16},{40,24},{48,32},{56,40},{64,... | collective-permute-start | bytes 1572872 | tf_op jit(solution)/shard_map/ppermute | solution.py:32
  4.4 45.6 %collective-permute-start.9 = (bf16[1024,512]{1,0:T(8,128)(2,1)}, bf16[1024,512]{1,0:T(8,128)(2,1)S(1)}, u32[]{:S(2)}, u32[]{:S(2)}) collective-permute-start(bf16[1024,512]{1,0:T(8,128)(2,1)} %param.8), channel_id=1, source_target_pairs={{0,8},{8,0},{16,24},{24,16},{32,40},{40,32},{48,56},{56,48},{64,72... | collective-permute-start | bytes 3145736 | tf_op jit(solution)/shard_map/ppermute | solution.py:36
  27.5 8.9 %collective-permute-start = (bf16[64,1024]{1,0:T(8,128)(2,1)}, bf16[64,1024]{1,0:T(8,128)(2,1)}, u32[]{:S(2)}, u32[]{:S(2)}) collective-permute-start(bf16[64,1024]{1,0:T(8,128)(2,1)} %get-tuple-element.11), channel_id=1, source_target_pairs={{0,8},{8,0},{16,24},{24,16},{32,40},{40,32},{48,56},{56,48},{64,72... | collective-permute-start | bytes 393224 | tf_op jit(solution)/shard_map/ppermute | solution.py:36
  27.7 13.2 %all-to-all-start = ((bf16[16,16,256]{2,1,0:T(8,128)(2,1)}), bf16[16,16,256]{2,1,0:T(8,128)(2,1)S(1)}, u32[]{:S(2)}, u32[]{:S(2)}) async-start(bf16[16,16,256]{2,1,0:T(8,128)(2,1)} %get-tuple-element.12), calls=%async_computation | async-start | bytes 262144 | tf_op jit(solution)/shard_map/all_to_all | solution.py:222
  35.0 14.9 %collective-permute-start.3 = (bf16[256,1024]{1,0:T(8,128)(2,1)S(1)}, bf16[256,1024]{1,0:T(8,128)(2,1)}, u32[]{:S(2)}, u32[]{:S(2)}) collective-permute-start(bf16[256,1024]{1,0:T(8,128)(2,1)S(1)} %collective-permute-done.1), channel_id=1, source_target_pairs={{0,16},{8,24},{16,32},{24,40},{32,48},{40,56},{48,64},{56,72},{64,... | collective-permute-start | bytes 1572872 | tf_op jit(solution)/shard_map/ppermute | solution.py:32
  41.4 14.4 %collective-permute-start.4 = (bf16[256,1024]{1,0:T(8,128)(2,1)}, bf16[256,1024]{1,0:T(8,128)(2,1)}, u32[]{:S(2)}, u32[]{:S(2)}) collective-permute-start(bf16[256,1024]{1,0:T(8,128)(2,1)} %collective-permute-done.2), channel_id=1, source_target_pairs={{0,112},{8,120},{16,0},{24,8},{32,16},{40,24},{48,32},{56,40},{64,... | collective-permute-start | bytes 1572872 | tf_op jit(solution)/shard_map/ppermute | solution.py:32
  42.4 73.7 %all-to-all-start.1 = ((bf16[8,4,16,256]{3,2,1,0:T(8,128)(2,1)}), bf16[8,4,16,256]{3,2,1,0:T(8,128)(2,1)S(1)}, u32[]{:S(2)}, u32[]{:S(2)}) async-start(bf16[8,4,16,256]{3,2,1,0:T(8,128)(2,1)} %broadcast_select_fusion), calls=%async_computation.1 | async-start | bytes 524288 | tf_op jit(solution)/shard_map/all_to_all | solution.py:224
  49.9 13.7 %collective-permute-start.5 = (bf16[256,1024]{1,0:T(8,128)(2,1)}, bf16[256,1024]{1,0:T(8,128)(2,1)S(1)}, u32[]{:S(2)}, u32[]{:S(2)}) collective-permute-start(bf16[256,1024]{1,0:T(8,128)(2,1)} %collective-permute-done.3), channel_id=1, source_target_pairs={{0,16},{8,24},{16,32},{24,40},{32,48},{40,56},{48,64},{56,72},{64,... | collective-permute-start | bytes 1572872 | tf_op jit(solution)/shard_map/ppermute | solution.py:32
  55.7 13.3 %collective-permute-start.6 = (bf16[256,1024]{1,0:T(8,128)(2,1)}, bf16[256,1024]{1,0:T(8,128)(2,1)S(1)}, u32[]{:S(2)}, u32[]{:S(2)}) collective-permute-start(bf16[256,1024]{1,0:T(8,128)(2,1)} %collective-permute-done.4), channel_id=1, source_target_pairs={{0,112},{8,120},{16,0},{24,8},{32,16},{40,24},{48,32},{56,40},{64,... | collective-permute-start | bytes 1572872 | tf_op jit(solution)/shard_map/ppermute | solution.py:32
  63.7 9.3 %collective-permute-start.7 = (bf16[128,1024]{1,0:T(8,128)(2,1)S(1)}, bf16[128,1024]{1,0:T(8,128)(2,1)S(1)}, u32[]{:S(2)}, u32[]{:S(2)}) collective-permute-start(bf16[128,1024]{1,0:T(8,128)(2,1)S(1)} %slice.98), channel_id=1, source_target_pairs={{0,16},{8,24},{16,32},{24,40},{32,48},{40,56},{48,64},{56,72},{64,... | collective-permute-start | bytes 786440 | tf_op jit(solution)/shard_map/ppermute | solution.py:32
  69.0 6.9 %collective-permute-start.8 = (bf16[128,1024]{1,0:T(8,128)(2,1)S(1)}, bf16[128,1024]{1,0:T(8,128)(2,1)S(1)}, u32[]{:S(2)}, u32[]{:S(2)}) collective-permute-start(bf16[128,1024]{1,0:T(8,128)(2,1)S(1)} %slice.99), channel_id=1, source_target_pairs={{0,112},{8,120},{16,0},{24,8},{32,16},{40,24},{48,32},{56,40},{64,... | collective-permute-start | bytes 786440 | tf_op jit(solution)/shard_map/ppermute | solution.py:32
  76.8 5.8 %collective-permute-start.10 = (bf16[128,1024]{1,0:T(8,128)(2,1)S(1)}, bf16[128,1024]{1,0:T(8,128)(2,1)S(1)}, u32[]{:S(2)}, u32[]{:S(2)}) collective-permute-start(bf16[128,1024]{1,0:T(8,128)(2,1)S(1)} %get-tuple-element.18), channel_id=1, source_target_pairs={{0,7},{1,0},{2,1},{3,2},{4,3},{5,4},{6,5},{7,6},{8,15},{9,8},{10,9... | collective-permute-start | bytes 786440 | tf_op jit(solution)/shard_map/ppermute | solution.py:40
  76.9 7.1 %collective-permute-start.14 = (bf16[128,1024]{1,0:T(8,128)(2,1)S(1)}, bf16[128,1024]{1,0:T(8,128)(2,1)S(1)}, u32[]{:S(2)}, u32[]{:S(2)}) collective-permute-start(bf16[128,1024]{1,0:T(8,128)(2,1)S(1)} %get-tuple-element.19), channel_id=1, source_target_pairs={{0,1},{1,2},{2,3},{3,4},{4,5},{5,6},{6,7},{7,0},{8,9},{9,10},{10,1... | collective-permute-start | bytes 786440 | tf_op jit(solution)/shard_map/ppermute | solution.py:40
  84.2 11.8 %collective-permute-start.15 = (bf16[256,1024]{1,0:T(8,128)(2,1)S(1)}, bf16[256,1024]{1,0:T(8,128)(2,1)S(1)}, u32[]{:S(2)}, u32[]{:S(2)}) collective-permute-start(bf16[256,1024]{1,0:T(8,128)(2,1)S(1)} %pad_maximum_fusion.1), channel_id=1, source_target_pairs={{0,1},{1,2},{2,3},{3,4},{4,5},{5,6},{6,7},{7,0},{8,9},{9,10},{10,1... | collective-permute-start | bytes 1572872 | tf_op jit(solution)/shard_map/ppermute | solution.py:40
  87.1 10.8 %collective-permute-start.11 = (bf16[256,1024]{1,0:T(8,128)(2,1)S(1)}, bf16[256,1024]{1,0:T(8,128)(2,1)S(1)}, u32[]{:S(2)}, u32[]{:S(2)}) collective-permute-start(bf16[256,1024]{1,0:T(8,128)(2,1)S(1)} %pad_maximum_fusion), channel_id=1, source_target_pairs={{0,7},{1,0},{2,1},{3,2},{4,3},{5,4},{6,5},{7,6},{8,15},{9,8},{10,9... | collective-permute-start | bytes 1572872 | tf_op jit(solution)/shard_map/ppermute | solution.py:40
  96.3 11.0 %collective-permute-start.16 = (bf16[256,1024]{1,0:T(8,128)(2,1)S(1)}, bf16[256,1024]{1,0:T(8,128)(2,1)S(1)}, u32[]{:S(2)}, u32[]{:S(2)}) collective-permute-start(bf16[256,1024]{1,0:T(8,128)(2,1)S(1)} %fusion.32), channel_id=1, source_target_pairs={{0,1},{1,2},{2,3},{3,4},{4,5},{5,6},{6,7},{7,0},{8,9},{9,10},{10,1... | collective-permute-start | bytes 1572872 | tf_op jit(solution)/shard_map/ppermute | solution.py:40
  107.6 15.0 %collective-permute-start.12 = (bf16[256,1024]{1,0:T(8,128)(2,1)S(1)}, bf16[256,1024]{1,0:T(8,128)(2,1)S(1)}, u32[]{:S(2)}, u32[]{:S(2)}) collective-permute-start(bf16[256,1024]{1,0:T(8,128)(2,1)S(1)} %get-tuple-element.16), channel_id=1, source_target_pairs={{0,7},{1,0},{2,1},{3,2},{4,3},{5,4},{6,5},{7,6},{8,15},{9,8},{10,9... | collective-permute-start | bytes 1572872 | tf_op jit(solution)/shard_map/ppermute | solution.py:40
  108.5 35.2 %collective-permute-start.18 = (bf16[256,512]{1,0:T(8,128)(2,1)S(1)}, bf16[256,512]{1,0:T(8,128)(2,1)}, u32[]{:S(2)}, u32[]{:S(2)}) collective-permute-start(bf16[256,512]{1,0:T(8,128)(2,1)S(1)} %get-tuple-element.27), channel_id=1, source_target_pairs={{0,8},{8,0},{16,24},{24,16},{32,40},{40,32},{48,56},{56,48},{64,72... | collective-permute-start | bytes 786440 | tf_op jit(solution)/shard_map/ppermute | solution.py:36
  116.1 10.5 %all-to-all-start.2 = ((bf16[8,16,256]{2,1,0:T(8,128)(2,1)}), bf16[8,16,256]{2,1,0:T(8,128)(2,1)S(1)}, u32[]{:S(2)}, u32[]{:S(2)}) async-start(bf16[8,16,256]{2,1,0:T(8,128)(2,1)} %shard_map.74), calls=%async_computation.2 | async-start | bytes 131072 | tf_op jit(solution)/shard_map/all_to_all | solution.py:266
  119.7 24.0 %collective-permute-start.17 = (bf16[256,512]{1,0:T(8,128)(2,1)S(1)}, bf16[256,512]{1,0:T(8,128)(2,1)S(1)}, u32[]{:S(2)}, u32[]{:S(2)}) collective-permute-start(bf16[256,512]{1,0:T(8,128)(2,1)S(1)} %get-tuple-element.24), channel_id=1, source_target_pairs={{0,1},{1,2},{2,3},{3,4},{4,5},{5,6},{6,7},{7,0},{8,9},{9,10},{10,1... | collective-permute-start | bytes 786440 | tf_op jit(solution)/shard_map/ppermute | solution.py:40
  121.4 22.3 %collective-permute-start.20 = (bf16[256,512]{1,0:T(8,128)(2,1)S(1)}, bf16[256,512]{1,0:T(8,128)(2,1)S(1)}, u32[]{:S(2)}, u32[]{:S(2)}) collective-permute-start(bf16[256,512]{1,0:T(8,128)(2,1)S(1)} %get-tuple-element.23), channel_id=1, source_target_pairs={{0,9},{1,10},{2,11},{3,12},{4,13},{5,14},{6,15},{7,8},{8,1},{9,2},... | collective-permute-start | bytes 786440 | tf_op jit(solution)/shard_map/ppermute | solution.py:49
  123.9 19.8 %collective-permute-start.13 = (bf16[256,512]{1,0:T(8,128)(2,1)S(1)}, bf16[256,512]{1,0:T(8,128)(2,1)S(1)}, u32[]{:S(2)}, u32[]{:S(2)}) collective-permute-start(bf16[256,512]{1,0:T(8,128)(2,1)S(1)} %get-tuple-element.26), channel_id=1, source_target_pairs={{0,7},{1,0},{2,1},{3,2},{4,3},{5,4},{6,5},{7,6},{8,15},{9,8},{10,9... | collective-permute-start | bytes 786440 | tf_op jit(solution)/shard_map/ppermute | solution.py:40
  125.7 18.1 %collective-permute-start.19 = (bf16[256,512]{1,0:T(8,128)(2,1)S(1)}, bf16[256,512]{1,0:T(8,128)(2,1)S(1)}, u32[]{:S(2)}, u32[]{:S(2)}) collective-permute-start(bf16[256,512]{1,0:T(8,128)(2,1)S(1)} %get-tuple-element.25), channel_id=1, source_target_pairs={{0,15},{1,8},{2,9},{3,10},{4,11},{5,12},{6,13},{7,14},{8,7},{9,0},... | collective-permute-start | bytes 786440 | tf_op jit(solution)/shard_map/ppermute | solution.py:49
  (10 other events, 84.1 us)

commit v2 on v1

--- a/solution.py
+++ b/solution.py
@@ -11,6 +11,7 @@
 BLOCK = 128
 CORES = 2
 CHUNKS = 1
+STREAMS = 1
 
 adapter_scale = 2.0
 
@@ -141,22 +142,6 @@
             u = up[seat * parts + h, b]
             e = lax.dot_general(s, u, (((0,), (0,)), ((), ())), preferred_element_type=f32)
             out[b * BLOCK : (b + 1) * BLOCK, h * part : (h + 1) * part] = adapter_scale * e
-
-
-def finish_kernel(chunks, *refs):
-    c_ref, extra = refs[0], refs[1]
-    out = refs[-1]
-    n = refs[2].shape[0]
-    rows = n * chunks
-    c = c_ref[0]
-    for q in range(chunks):
-        own, dn_own, up_own, oth, dn_oth, up_oth = refs[2 + 6 * q : 8 + 6 * q]
-        at = pl.multiple_of(c * rows + q * n, n)
-        v = own[...].astype(f32) + dn_own[...].astype(f32) + up_own[...].astype(f32)
-        out[pl.ds(at, n)] = (v + extra[pl.ds(at, n)]).astype(bf16)
-        at = pl.multiple_of((1 - c) * rows + q * n, n)
-        v = oth[...].astype(f32) + dn_oth[...].astype(f32) + up_oth[...].astype(f32)
-        out[pl.ds(at, n)] = (v + extra[pl.ds(at, n)]).astype(bf16)
 
 
 def on_device(
@@ -220,10 +205,8 @@
     down_oth = swap_cores(down_own, chips)
     down_chip = jnp.concatenate([down_own, down_oth], axis=0)
     up_part = lax.all_to_all(up_part, "adapter", 0, 0, tiled=True)
-    up_all = jnp.take(up_part, table[0], axis=0)
-    up_all = lax.all_to_all(
-        up_all.reshape(slices, blk_chip, rank, part), "tensor", 0, 0, tiled=True
-    )
+    up_all = jnp.take(up_part, table[0], axis=0).reshape(slices, blk_chip, rank, part)
+    up_all = lax.all_to_all(up_all, "tensor", 0, 0, tiled=True)
 
     shr_buf = jnp.zeros((chips, CORES * seats * rank, rows), bf16)
     bufs = []
@@ -255,68 +238,78 @@
             ups[q].append(shift_chips(up, chips, 1))
             dns[q].append(shift_chips(dn, chips, -1))
 
-    shr = pl.pallas_call(
+    pick = pl.pallas_call(
         functools.partial(pick_kernel, rank, blk_dev),
+        name="pick",
         out_shape=jax.ShapeDtypeStruct((chips, rank, rows), bf16),
         in_specs=[SMEM, SMEM, VMEM],
         out_specs=VMEM,
         cost_estimate=pl.CostEstimate(flops=10**7, bytes_accessed=10**6, transcendentals=0),
-    )(table, c[None], shr_buf)
+    )
+    shr = pick(table, c[None], shr_buf)
     shr, up_all = lax.optimization_barrier((shr, up_all))
     shr = lax.all_to_all(shr, "tensor", 0, 0, tiled=True)
     shr = jnp.sum(shr.astype(f32), axis=0).astype(bf16)
     shr = jnp.broadcast_to(shr[None], (owners, rank, rows))
     shr = lax.all_to_all(shr, "adapter", 0, 0, tiled=True)
-    extra = pl.pallas_call(
+    expand = pl.pallas_call(
         functools.partial(extra_kernel, blk_dev),
+        name="extra",
         out_shape=jax.ShapeDtypeStruct((blk_chip * BLOCK, cols), f32),
         in_specs=[SMEM, VMEM, VMEM, SMEM],
         out_specs=VMEM,
         cost_estimate=pl.CostEstimate(flops=10**7, bytes_accessed=10**6, transcendentals=0),
-    )(table, shr, up_all, y[None])
-
-    def mine(q, t):
-        return lax.dynamic_index_in_dim(bufs[q], t % slices, 0, keepdims=False)
-
-    m = n // 2
-    dn, up = [], []
-    for q in range(CHUNKS):
-        far = mine(q, y + half)
-        dn.append(shift_slices(far[:m], slices, -1))
-        up.append(shift_slices(far[m:], slices, 1))
-    ends = []
+    )
+    extra = expand(table, shr, up_all, y[None])
+
+    k = rows // STREAMS
+    m = k // 2
+
+    def mine(t, lo, size):
+        return lax.dynamic_slice(bufs[0], (t % slices, lo, 0), (1, size, CORES * cols))[0]
+
+    dn, up, ends = [], [], []
+    for r in range(STREAMS):
+        dn.append(shift_slices(mine(y + half, r * k, m), slices, -1))
+        up.append(shift_slices(mine(y + half, r * k + m, m), slices, 1))
+    last = mine(y, 0, rows)
+    oth = swap_cores(last[:, cols:], chips)
+    before = None
     for h in range(half - 1, 0, -1):
-        for q in range(CHUNKS):
-            d = mine(q, y + slices - h).astype(f32)
-            u = mine(q, y + h).astype(f32)
+        for r in range(STREAMS):
+            if before is None:
+                dn[r], up[r] = lax.optimization_barrier((dn[r], up[r]))
+            else:
+                dn[r], up[r], before = lax.optimization_barrier((dn[r], up[r], before))
+            d = mine(y + slices - h, r * k, k).astype(f32)
+            u = mine(y + h, r * k, k).astype(f32)
             if h == half - 1:
-                d = jnp.concatenate([d[:m] + dn[q].astype(f32), d[m:]], axis=0)
-                u = jnp.concatenate([u[:m], u[m:] + up[q].astype(f32)], axis=0)
+                d = jnp.concatenate([d[:m] + dn[r].astype(f32), d[m:]], axis=0)
+                u = jnp.concatenate([u[:m], u[m:] + up[r].astype(f32)], axis=0)
             else:
-                d = d + dn[q].astype(f32)
-                u = u + up[q].astype(f32)
+                d = d + dn[r].astype(f32)
+                u = u + up[r].astype(f32)
             d, u = d.astype(bf16), u.astype(bf16)
-            if h > 1:
-                dn[q] = shift_slices(d, slices, -1)
-                up[q] = shift_slices(u, slices, 1)
-            else:
-                last = mine(q, y)
-                oth = swap_cores(last[:, cols:], chips)
-                ends += [
-                    last[:, :cols],
-                    shift_slices(d[:, :cols], slices, -1),
-                    shift_slices(u[:, :cols], slices, 1),
-                    oth,
-                    shift_slices_swap(d[:, cols:], owners, slices, -1),
-                    shift_slices_swap(u[:, cols:], owners, slices, 1),
-                ]
-    return pl.pallas_call(
-        functools.partial(finish_kernel, CHUNKS),
-        out_shape=jax.ShapeDtypeStruct((CORES * rows, cols), bf16),
-        in_specs=[SMEM] + [VMEM] * (1 + 6 * CHUNKS),
-        out_specs=VMEM,
-        cost_estimate=pl.CostEstimate(flops=10**7, bytes_accessed=10**6, transcendentals=0),
-    )(c[None], extra, *ends)
+            if h == 1:
+                d, dx = d[:, :cols], d[:, cols:]
+                u, ux = u[:, :cols], u[:, cols:]
+            before = d
+            dn[r] = shift_slices(d, slices, -1)
+            up[r] = shift_slices(u, slices, 1)
+            if h == 1:
+                dx = shift_slices_swap(dx, owners, slices, -1)
+                ux = shift_slices_swap(ux, owners, slices, 1)
+                ends += [dn[r], up[r], dx, ux]
+    out = []
+    order = lax.broadcasted_iota(i32, (CORES, k, cols), 0)
+    extra = extra.reshape(CORES, rows, cols)
+    for r in range(STREAMS):
+        sums = [v.astype(f32)[None] for v in ends[4 * r : 4 * r + 4]]
+        v_own = last[r * k : (r + 1) * k, :cols].astype(f32)[None] + sums[0] + sums[1]
+        v_oth = oth[r * k : (r + 1) * k].astype(f32)[None] + sums[2] + sums[3]
+        v = jnp.where(order == c, v_own, v_oth) + extra[:, r * k : (r + 1) * k]
+        out.append(v.astype(bf16))
+    return jnp.concatenate(out, axis=1).reshape(CORES * rows, cols)
 
 
 def solution(mesh):

time: 148 us -> 153 us (1.034)
  starting transfers between devices: 54.6 us -> 70.7 us
  blocking collectives: 14.7 us -> 0 us
  other arithmetic: 4.27 us -> 10.4 us
  local copies, waits for them, and re-layouts: 9.87 us -> 14.5 us
  waiting for transfers between devices: 39.2 us -> 35.2 us
  Pallas kernels: 9.92 us -> 7.25 us
    all_to_all x1 -> x0, blocking collectives: 14.7 us -> none  [on_device(): shr = lax.all_to_all(shr, 'adapter', 0, 0, tiled=True)]
    all_to_all x1 -> x2, starting transfers between devices: 3.62 us -> 15 us  [the longest x1 11.4 us: on_device(): shr = lax.all_to_all(shr, 'adapter', 0, 0, tiled=True)]
    ppermute x8, waiting for transfers between devices: 20.3 us -> 11.6 us  [shift_slices(): lax.ppermute(v, 'tensor', [(y, (y + step) % slices) for y in range(slices)])]
    all_to_all x1 -> x2, waiting for transfers between devices: 0.01 us -> 5.49 us  [the longest x1 5.48 us: on_device(): shr = lax.all_to_all(shr, 'adapter', 0, 0, tiled=True)]
    ppermute x8, starting transfers between devices: 9.82 us -> 14.3 us  [shift_chips(): return lax.ppermute(v, 'adapter', pairs)]
    ppermute x3, starting transfers between devices: 24.1 us -> 19.9 us  [swap_cores(): lax.ppermute(v, 'adapter', [(i, i ^ 1) for i in range(chips * CORES)])]
    pallas_call x3 -> x2, Pallas kernels: 6.75 us -> 4.09 us  [the longest x1 2.34 us: on_device(): extra = expand(table, shr, up_all, y[None])]
    convert_element_type x3 -> x2, other arithmetic: 1.83 us -> 4.37 us  [on_device(): d, u = (d.astype(bf16), u.astype(bf16))]
  transfers between devices with their start and end apart: 24 -> 25, of which waited for: 12 -> 9; matrix products, arithmetic and copies ran while one was open for 17% -> 20% of each run, Pallas kernels for 5% -> 5%
where the time goes in v2:
time: 153 us; the launch traced here: 152 us
  starting transfers between devices  70.7 us (46%)
  waiting for transfers between devices  35.2 us (23%)
  local copies, waits for them, and re-layouts  14.5 us (9%)
  matrix products  13.5 us (9%)
  other arithmetic  10.4 us (7%)
  Pallas kernels  7.25 us (5%)
    ppermute x3, starting transfers between devices, swap_cores(): lax.ppermute(v, 'adapter', [(i, i ^ 1) for i in range(chips * CORES)])  19.9 us
    ppermute x8, waiting for transfers between devices, shift_chips(): return lax.ppermute(v, 'adapter', pairs)  16 us
    ppermute x8, starting transfers between devices, shift_chips(): return lax.ppermute(v, 'adapter', pairs)  14.3 us
    ppermute x8, waiting for transfers between devices, shift_slices(): lax.ppermute(v, 'tensor', [(y, (y + step) % slices) for y in range(slices)])  11.6 us
    all_to_all x1, starting transfers between devices, on_device(): shr = lax.all_to_all(shr, 'adapter', 0, 0, tiled=True)  11.4 us
    ppermute x8, starting transfers between devices, shift_slices(): lax.ppermute(v, 'tensor', [(y, (y + step) % slices) for y in range(slices)])  10.7 us
    dot_general x8, matrix products, put(): p = jnp.dot(tok, w_both, preferred_element_type=f32).astype(bf16)  7.77 us
    unnamed x23, local copies, waits for them, and re-layouts  6.59 us
  transfers between devices with their start and end apart: 25, of which 9 were waited for; matrix products, arithmetic and copies ran while one was open for 20% of the time, Pallas kernels for 5%

profile of v2, /device:TPU:513, one launch (start us, length us, event | category | flops | bytes accessed | tf_op | source)
XLA Modules:
  0.0 151.9 jit_solution(5911143995207460438)
XLA Ops:
  0.0 2.2 %collective-permute-start.1 = (bf16[256,1024]{1,0:T(8,128)(2,1)}, bf16[256,1024]{1,0:T(8,128)(2,1)S(1)}, u32[]{:S(2)}, u32[]{:S(2)}) collective-permute-start(bf16[256,1024]{1,0:T(8,128)(2,1)} %param.7), channel_id=1, source_target_pairs={{0,16},{8,24},{16,32},{24,40},{32,48},{40,56},{48,64},{56,72},{64,... | collective-permute-start | bytes 1572872 | tf_op jit(solution)/shard_map/ppermute | solution.py:33
  2.2 2.2 %collective-permute-start.2 = (bf16[256,1024]{1,0:T(8,128)(2,1)}, bf16[256,1024]{1,0:T(8,128)(2,1)S(1)}, u32[]{:S(2)}, u32[]{:S(2)}) collective-permute-start(bf16[256,1024]{1,0:T(8,128)(2,1)} %param.7), channel_id=1, source_target_pairs={{0,112},{8,120},{16,0},{24,8},{32,16},{40,24},{48,32},{56,40},{64,... | collective-permute-start | bytes 1572872 | tf_op jit(solution)/shard_map/ppermute | solution.py:33
  4.4 19.3 %collective-permute-start = (bf16[1024,512]{1,0:T(8,128)(2,1)}, bf16[1024,512]{1,0:T(8,128)(2,1)}, u32[]{:S(2)}, u32[]{:S(2)}) collective-permute-start(bf16[1024,512]{1,0:T(8,128)(2,1)} %param.8), channel_id=1, source_target_pairs={{0,8},{8,0},{16,24},{24,16},{32,40},{40,32},{48,56},{56,48},{64,72... | collective-permute-start | bytes 3145736 | tf_op jit(solution)/shard_map/ppermute | solution.py:37
  24.2 3.2 %shard_map.73 = (s32[4,32]{1,0:T(4,128)}, bf16[64,1024]{1,0:T(8,128)(2,1)}, bf16[16,16,256]{2,1,0:T(8,128)(2,1)}) custom-call(s32[2]{0:T(128)} %pad_add_fusion.where, s32[32]{0:T(128)} %ids.1, s32[32]{0:T(128)} %live.1, s32[512]{0:T(512)} %index.1, bf16[32,16,1024]{2,1,0:T(8,128)(2,1)} %down.1, bf16[32,16,8192]{2,1,0:T(8,128)(2,1)} %up.1), custom_call_target="tpu_custom_call" | custom-call | flops 10000000 | bytes 1000000 | tf_op jit(solution)/shard_map/pallas_call | solution.py:182
  27.6 3.8 %all-to-all-start = ((bf16[16,16,256]{2,1,0:T(8,128)(2,1)}), bf16[16,16,256]{2,1,0:T(8,128)(2,1)S(1)}, u32[]{:S(2)}, u32[]{:S(2)}) async-start(bf16[16,16,256]{2,1,0:T(8,128)(2,1)} %get-tuple-element.24), calls=%async_computation | async-start | bytes 262144 | tf_op jit(solution)/shard_map/all_to_all | solution.py:207
  36.4 1.9 %collective-permute-start.4 = (bf16[256,1024]{1,0:T(8,128)(2,1)S(1)}, bf16[256,1024]{1,0:T(8,128)(2,1)}, u32[]{:S(2)}, u32[]{:S(2)}) collective-permute-start(bf16[256,1024]{1,0:T(8,128)(2,1)S(1)} %collective-permute-done.2), channel_id=1, source_target_pairs={{0,112},{8,120},{16,0},{24,8},{32,16},{40,24},{48,32},{56,40},{64,... | collective-permute-start | bytes 1572872 | tf_op jit(solution)/shard_map/ppermute | solution.py:33
  38.7 2.0 %all-to-all-done = bf16[16,16,256]{2,1,0:T(8,128)(2,1)S(1)} async-done(((bf16[16,16,256]{2,1,0:T(8,128)(2,1)}), bf16[16,16,256]{2,1,0:T(8,128)(2,1)S(1)}, u32[]{:S(2)}, u32[]{:S(2)}) %all-to-all-start) | async-done | bytes 131104 | tf_op jit(solution)/shard_map/all_to_all | solution.py:207
  41.3 8.4 %collective-permute-done.3 = bf16[256,1024]{1,0:T(8,128)(2,1)} collective-permute-done((bf16[256,1024]{1,0:T(8,128)(2,1)S(1)}, bf16[256,1024]{1,0:T(8,128)(2,1)}, u32[]{:S(2)}, u32[]{:S(2)}) %collective-permute-start.3) | collective-permute-done | bytes 524320 | tf_op jit(solution)/shard_map/ppermute | solution.py:33
  49.7 2.4 %constant_dynamic-update-slice_fusion = bf16[1024,1024]{1,0:T(8,128)(2,1)} fusion(bf16[1024,1024]{1,0:T(8,128)(2,1)} %constant_dynamic-update-slice_fusion.1, bf16[1024,512]{1,0:T(8,128)(2,1)} %collective-permute-done), kind=kLoop, calls=%fused_computation.76 | loop fusion | bytes 2097152 | tf_op jit(solution)/shard_map/concatenate | solution.py:180
  54.3 2.8 %collective-permute-start.6 = (bf16[256,1024]{1,0:T(8,128)(2,1)}, bf16[256,1024]{1,0:T(8,128)(2,1)S(1)}, u32[]{:S(2)}, u32[]{:S(2)}) collective-permute-start(bf16[256,1024]{1,0:T(8,128)(2,1)} %collective-permute-done.4), channel_id=1, source_target_pairs={{0,112},{8,120},{16,0},{24,8},{32,16},{40,24},{48,32},{56,40},{64,... | collective-permute-start | bytes 1572872 | tf_op jit(solution)/shard_map/ppermute | solution.py:33
  63.9 3.7 %collective-permute-done.6 = bf16[256,1024]{1,0:T(8,128)(2,1)S(1)} collective-permute-done((bf16[256,1024]{1,0:T(8,128)(2,1)}, bf16[256,1024]{1,0:T(8,128)(2,1)S(1)}, u32[]{:S(2)}, u32[]{:S(2)}) %collective-permute-start.6) | collective-permute-done | bytes 524320 | tf_op jit(solution)/shard_map/ppermute | solution.py:33
  67.7 3.6 %collective-permute-start.8 = (bf16[128,1024]{1,0:T(8,128)(2,1)S(1)}, bf16[128,1024]{1,0:T(8,128)(2,1)S(1)}, u32[]{:S(2)}, u32[]{:S(2)}) collective-permute-start(bf16[128,1024]{1,0:T(8,128)(2,1)S(1)} %slice.83), channel_id=1, source_target_pairs={{0,112},{8,120},{16,0},{24,8},{32,16},{40,24},{48,32},{56,40},{64,... | collective-permute-start | bytes 786440 | tf_op jit(solution)/shard_map/ppermute | solution.py:33
  72.7 2.2 %collective-permute-done.8 = bf16[128,1024]{1,0:T(8,128)(2,1)S(1)} collective-permute-done((bf16[128,1024]{1,0:T(8,128)(2,1)S(1)}, bf16[128,1024]{1,0:T(8,128)(2,1)S(1)}, u32[]{:S(2)}, u32[]{:S(2)}) %collective-permute-start.8) | collective-permute-done | bytes 262176 | tf_op jit(solution)/shard_map/ppermute | solution.py:33
  75.7 2.0 %copy-done = bf16[8,256,1024]{2,1,0:T(8,128)(2,1)} copy-done((bf16[8,256,1024]{2,1,0:T(8,128)(2,1)}, bf16[8,256,1024]{2,1,0:T(8,128)(2,1)S(1)}, u32[]{:S(2)}) %copy-start) | copy-done | bytes 4194328
  78.6 2.7 %collective-permute-start.9 = (bf16[128,1024]{1,0:T(8,128)(2,1)}, bf16[128,1024]{1,0:T(8,128)(2,1)}, u32[]{:S(2)}, u32[]{:S(2)}) collective-permute-start(bf16[128,1024]{1,0:T(8,128)(2,1)} %get-tuple-element.33), channel_id=1, source_target_pairs={{0,7},{1,0},{2,1},{3,2},{4,3},{5,4},{6,5},{7,6},{8,15},{9,8},{10,9... | collective-permute-start | bytes 786440 | tf_op jit(solution)/shard_map/ppermute | solution.py:41
  82.1 3.6 %all-to-all-start.1 = ((bf16[8,4,16,256]{3,2,1,0:T(8,128)(2,1)}), bf16[8,4,16,256]{3,2,1,0:T(8,128)(2,1)S(1)}, u32[]{:S(2)}, u32[]{:S(2)}) async-start(bf16[8,4,16,256]{3,2,1,0:T(8,128)(2,1)} %broadcast_select_fusion), calls=%async_computation.1 | async-start | bytes 524288 | tf_op jit(solution)/shard_map/all_to_all | solution.py:209
  94.6 9.8 %collective-permute-done.12 = bf16[256,1024]{1,0:T(8,128)(2,1)S(1)} collective-permute-done((bf16[256,1024]{1,0:T(8,128)(2,1)S(1)}, bf16[256,1024]{1,0:T(8,128)(2,1)S(1)}, u32[]{:S(2)}, u32[]{:S(2)}) %collective-permute-start.12) | collective-permute-done | bytes 524320 | tf_op jit(solution)/shard_map/ppermute | solution.py:41
  104.4 2.6 %fusion.33 = (bf16[256,1024]{1,0:T(8,128)(2,1)}, bf16[256,1024]{1,0:T(8,128)(2,1)}) fusion(bf16[256,1024]{1,0:T(8,128)(2,1)S(1)} %collective-permute-done.12, bf16[8,256,1024]{2,1,0:T(8,128)(2,1)} %copy-done, s32[]{:T(128)S(6)} %select_n.192, bf16[256,1024]{1,0:T(8,128)(2,1)S(1)} %collective-permute-done.11, s32[]{:T(128)S(6)} %select_n.184), kind=kLoop, calls=%fused_computation.52 | loop fusion | flops 2097152 | bytes 3145736 | tf_op jit(solution)/shard_map/convert_element_type | solution.py:292
  112.4 5.3 %all-to-all-start.2 = ((bf16[8,16,256]{2,1,0:T(8,128)(2,1)}), bf16[8,16,256]{2,1,0:T(8,128)(2,1)S(1)}, u32[]{:S(2)}, u32[]{:S(2)}) async-start(bf16[8,16,256]{2,1,0:T(8,128)(2,1)} %pick.1), calls=%async_computation.2 | async-start | bytes 131072 | tf_op jit(solution)/shard_map/all_to_all | solution.py:251
  121.4 3.2 %collective-permute-start.15 = (bf16[256,512]{1,0:T(8,128)(2,1)S(1)}, bf16[256,512]{1,0:T(8,128)(2,1)S(1)}, u32[]{:S(2)}, u32[]{:S(2)}) collective-permute-start(bf16[256,512]{1,0:T(8,128)(2,1)S(1)} %get-tuple-element.37), channel_id=1, source_target_pairs={{0,7},{1,0},{2,1},{3,2},{4,3},{5,4},{6,5},{7,6},{8,15},{9,8},{10,9... | collective-permute-start | bytes 786440 | tf_op jit(solution)/shard_map/ppermute | solution.py:41
  126.0 11.4 %all-to-all-start.3 = ((bf16[16,16,256]{2,1,0:T(8,128)(2,1)}), bf16[16,16,256]{2,1,0:T(8,128)(2,1)S(1)}, u32[]{:S(2)}, u32[]{:S(2)}) async-start(bf16[16,16,256]{2,1,0:T(8,128)(2,1)} %broadcast_in_dim.125), calls=%async_computation.3 | async-start | bytes 262144 | tf_op jit(solution)/shard_map/all_to_all | solution.py:254
  140.8 5.5 %all-to-all-done.3.shr = bf16[16,16,256]{2,1,0:T(8,128)(2,1)S(1)} async-done(((bf16[16,16,256]{2,1,0:T(8,128)(2,1)}), bf16[16,16,256]{2,1,0:T(8,128)(2,1)S(1)}, u32[]{:S(2)}, u32[]{:S(2)}) %all-to-all-start.3) | async-done | bytes 131104 | tf_op jit(solution)/shard_map/all_to_all | solution.py:254
  147.0 2.3 %extra.1 = f32[512,512]{1,0:T(8,128)} custom-call(s32[4,32]{1,0:T(4,128)} %get-tuple-element.22.table, bf16[16,16,256]{2,1,0:T(8,128)(2,1)} %copy-done.9, bf16[8,4,16,256]{3,2,1,0:T(8,128)(2,1)} %copy-done.3, s32[1]{0:T(128)} %bitcast.29.y_ref), custom_call_target="tpu_custom_call" | custom-call | flops 10000000 | bytes 1000000 | tf_op jit(solution)/shard_map/extra/pallas_call | solution.py:263
  149.6 2.3 %fusion.37 = bf16[512,512]{1,0:T(8,128)(2,1)} fusion(f32[512,512]{1,0:T(8,128)} %extra.1, f32[256,512]{1,0:T(8,128)S(1)} %convert_add_fusion.6, f32[256,512]{1,0:T(8,128)S(1)} %convert_add_fusion.7, pred[512]{0:T(512)(128)(4,1)S(1)} %iota.12), kind=kLoop, calls=%fused_computation.59 | loop fusion | flops 786432 | bytes 2621952 | tf_op jit(solution)/shard_map/convert_element_type | solution.py:311
  (101 shorter events, 43.1 us)
Async XLA Ops:
  0.0 33.7 %collective-permute-start.1 = (bf16[256,1024]{1,0:T(8,128)(2,1)}, bf16[256,1024]{1,0:T(8,128)(2,1)S(1)}, u32[]{:S(2)}, u32[]{:S(2)}) collective-permute-start(bf16[256,1024]{1,0:T(8,128)(2,1)} %param.7), channel_id=1, source_target_pairs={{0,16},{8,24},{16,32},{24,40},{32,48},{40,56},{48,64},{56,72},{64,... | collective-permute-start | bytes 1572872 | tf_op jit(solution)/shard_map/ppermute | solution.py:33
  2.2 34.3 %collective-permute-start.2 = (bf16[256,1024]{1,0:T(8,128)(2,1)}, bf16[256,1024]{1,0:T(8,128)(2,1)S(1)}, u32[]{:S(2)}, u32[]{:S(2)}) collective-permute-start(bf16[256,1024]{1,0:T(8,128)(2,1)} %param.7), channel_id=1, source_target_pairs={{0,112},{8,120},{16,0},{24,8},{32,16},{40,24},{48,32},{56,40},{64,... | collective-permute-start | bytes 1572872 | tf_op jit(solution)/shard_map/ppermute | solution.py:33
  4.4 45.3 %collective-permute-start = (bf16[1024,512]{1,0:T(8,128)(2,1)}, bf16[1024,512]{1,0:T(8,128)(2,1)}, u32[]{:S(2)}, u32[]{:S(2)}) collective-permute-start(bf16[1024,512]{1,0:T(8,128)(2,1)} %param.8), channel_id=1, source_target_pairs={{0,8},{8,0},{16,24},{24,16},{32,40},{40,32},{48,56},{56,48},{64,72... | collective-permute-start | bytes 3145736 | tf_op jit(solution)/shard_map/ppermute | solution.py:37
  27.4 9.0 %collective-permute-start.20 = (bf16[64,1024]{1,0:T(8,128)(2,1)}, bf16[64,1024]{1,0:T(8,128)(2,1)S(1)}, u32[]{:S(2)}, u32[]{:S(2)}) collective-permute-start(bf16[64,1024]{1,0:T(8,128)(2,1)} %get-tuple-element.23), channel_id=1, source_target_pairs={{0,8},{8,0},{16,24},{24,16},{32,40},{40,32},{48,56},{56,48},{64,72... | collective-permute-start | bytes 393224 | tf_op jit(solution)/shard_map/ppermute | solution.py:37
  27.6 13.1 %all-to-all-start = ((bf16[16,16,256]{2,1,0:T(8,128)(2,1)}), bf16[16,16,256]{2,1,0:T(8,128)(2,1)S(1)}, u32[]{:S(2)}, u32[]{:S(2)}) async-start(bf16[16,16,256]{2,1,0:T(8,128)(2,1)} %get-tuple-element.24), calls=%async_computation | async-start | bytes 262144 | tf_op jit(solution)/shard_map/all_to_all | solution.py:207
  33.7 15.9 %collective-permute-start.3 = (bf16[256,1024]{1,0:T(8,128)(2,1)S(1)}, bf16[256,1024]{1,0:T(8,128)(2,1)}, u32[]{:S(2)}, u32[]{:S(2)}) collective-permute-start(bf16[256,1024]{1,0:T(8,128)(2,1)S(1)} %collective-permute-done.1), channel_id=1, source_target_pairs={{0,16},{8,24},{16,32},{24,40},{32,48},{40,56},{48,64},{56,72},{64,... | collective-permute-start | bytes 1572872 | tf_op jit(solution)/shard_map/ppermute | solution.py:33
  36.4 17.9 %collective-permute-start.4 = (bf16[256,1024]{1,0:T(8,128)(2,1)S(1)}, bf16[256,1024]{1,0:T(8,128)(2,1)}, u32[]{:S(2)}, u32[]{:S(2)}) collective-permute-start(bf16[256,1024]{1,0:T(8,128)(2,1)S(1)} %collective-permute-done.2), channel_id=1, source_target_pairs={{0,112},{8,120},{16,0},{24,8},{32,16},{40,24},{48,32},{56,40},{64,... | collective-permute-start | bytes 1572872 | tf_op jit(solution)/shard_map/ppermute | solution.py:33
  49.7 14.1 %collective-permute-start.5 = (bf16[256,1024]{1,0:T(8,128)(2,1)}, bf16[256,1024]{1,0:T(8,128)(2,1)S(1)}, u32[]{:S(2)}, u32[]{:S(2)}) collective-permute-start(bf16[256,1024]{1,0:T(8,128)(2,1)} %collective-permute-done.3), channel_id=1, source_target_pairs={{0,16},{8,24},{16,32},{24,40},{32,48},{40,56},{48,64},{56,72},{64,... | collective-permute-start | bytes 1572872 | tf_op jit(solution)/shard_map/ppermute | solution.py:33
  54.3 13.3 %collective-permute-start.6 = (bf16[256,1024]{1,0:T(8,128)(2,1)}, bf16[256,1024]{1,0:T(8,128)(2,1)S(1)}, u32[]{:S(2)}, u32[]{:S(2)}) collective-permute-start(bf16[256,1024]{1,0:T(8,128)(2,1)} %collective-permute-done.4), channel_id=1, source_target_pairs={{0,112},{8,120},{16,0},{24,8},{32,16},{40,24},{48,32},{56,40},{64,... | collective-permute-start | bytes 1572872 | tf_op jit(solution)/shard_map/ppermute | solution.py:33
  63.8 8.9 %collective-permute-start.7 = (bf16[128,1024]{1,0:T(8,128)(2,1)S(1)}, bf16[128,1024]{1,0:T(8,128)(2,1)S(1)}, u32[]{:S(2)}, u32[]{:S(2)}) collective-permute-start(bf16[128,1024]{1,0:T(8,128)(2,1)S(1)} %slice.82), channel_id=1, source_target_pairs={{0,16},{8,24},{16,32},{24,40},{32,48},{40,56},{48,64},{56,72},{64,... | collective-permute-start | bytes 786440 | tf_op jit(solution)/shard_map/ppermute | solution.py:33
  78.6 8.5 %collective-permute-start.10 = (bf16[128,1024]{1,0:T(8,128)(2,1)}, bf16[128,1024]{1,0:T(8,128)(2,1)}, u32[]{:S(2)}, u32[]{:S(2)}) collective-permute-start(bf16[128,1024]{1,0:T(8,128)(2,1)} %get-tuple-element.32), channel_id=1, source_target_pairs={{0,1},{1,2},{2,3},{3,4},{4,5},{5,6},{6,7},{7,0},{8,9},{9,10},{10,1... | collective-permute-start | bytes 786440 | tf_op jit(solution)/shard_map/ppermute | solution.py:41
  78.6 8.5 %collective-permute-start.9 = (bf16[128,1024]{1,0:T(8,128)(2,1)}, bf16[128,1024]{1,0:T(8,128)(2,1)}, u32[]{:S(2)}, u32[]{:S(2)}) collective-permute-start(bf16[128,1024]{1,0:T(8,128)(2,1)} %get-tuple-element.33), channel_id=1, source_target_pairs={{0,7},{1,0},{2,1},{3,2},{4,3},{5,4},{6,5},{7,6},{8,15},{9,8},{10,9... | collective-permute-start | bytes 786440 | tf_op jit(solution)/shard_map/ppermute | solution.py:41
  82.1 30.3 %all-to-all-start.1 = ((bf16[8,4,16,256]{3,2,1,0:T(8,128)(2,1)}), bf16[8,4,16,256]{3,2,1,0:T(8,128)(2,1)S(1)}, u32[]{:S(2)}, u32[]{:S(2)}) async-start(bf16[8,4,16,256]{3,2,1,0:T(8,128)(2,1)} %broadcast_select_fusion), calls=%async_computation.1 | async-start | bytes 524288 | tf_op jit(solution)/shard_map/all_to_all | solution.py:209
  88.6 15.8 %collective-permute-start.12 = (bf16[256,1024]{1,0:T(8,128)(2,1)S(1)}, bf16[256,1024]{1,0:T(8,128)(2,1)S(1)}, u32[]{:S(2)}, u32[]{:S(2)}) collective-permute-start(bf16[256,1024]{1,0:T(8,128)(2,1)S(1)} %pad_maximum_fusion.1), channel_id=1, source_target_pairs={{0,1},{1,2},{2,3},{3,4},{4,5},{5,6},{6,7},{7,0},{8,9},{9,10},{10,1... | collective-permute-start | bytes 1572872 | tf_op jit(solution)/shard_map/ppermute | solution.py:41
  89.9 14.5 %collective-permute-start.11 = (bf16[256,1024]{1,0:T(8,128)(2,1)S(1)}, bf16[256,1024]{1,0:T(8,128)(2,1)S(1)}, u32[]{:S(2)}, u32[]{:S(2)}) collective-permute-start(bf16[256,1024]{1,0:T(8,128)(2,1)S(1)} %pad_maximum_fusion), channel_id=1, source_target_pairs={{0,7},{1,0},{2,1},{3,2},{4,3},{5,4},{6,5},{7,6},{8,15},{9,8},{10,9... | collective-permute-start | bytes 1572872 | tf_op jit(solution)/shard_map/ppermute | solution.py:41
  107.0 11.5 %collective-permute-start.13 = (bf16[256,1024]{1,0:T(8,128)(2,1)}, bf16[256,1024]{1,0:T(8,128)(2,1)S(1)}, u32[]{:S(2)}, u32[]{:S(2)}) collective-permute-start(bf16[256,1024]{1,0:T(8,128)(2,1)} %get-tuple-element.30), channel_id=1, source_target_pairs={{0,7},{1,0},{2,1},{3,2},{4,3},{5,4},{6,5},{7,6},{8,15},{9,8},{10,9... | collective-permute-start | bytes 1572872 | tf_op jit(solution)/shard_map/ppermute | solution.py:41
  107.9 11.7 %collective-permute-start.14 = (bf16[256,1024]{1,0:T(8,128)(2,1)}, bf16[256,1024]{1,0:T(8,128)(2,1)}, u32[]{:S(2)}, u32[]{:S(2)}) collective-permute-start(bf16[256,1024]{1,0:T(8,128)(2,1)} %get-tuple-element.29), channel_id=1, source_target_pairs={{0,1},{1,2},{2,3},{3,4},{4,5},{5,6},{6,7},{7,0},{8,9},{9,10},{10,1... | collective-permute-start | bytes 1572872 | tf_op jit(solution)/shard_map/ppermute | solution.py:41
  112.4 12.9 %all-to-all-start.2 = ((bf16[8,16,256]{2,1,0:T(8,128)(2,1)}), bf16[8,16,256]{2,1,0:T(8,128)(2,1)S(1)}, u32[]{:S(2)}, u32[]{:S(2)}) async-start(bf16[8,16,256]{2,1,0:T(8,128)(2,1)} %pick.1), calls=%async_computation.2 | async-start | bytes 131072 | tf_op jit(solution)/shard_map/all_to_all | solution.py:251
  121.4 28.0 %collective-permute-start.15 = (bf16[256,512]{1,0:T(8,128)(2,1)S(1)}, bf16[256,512]{1,0:T(8,128)(2,1)S(1)}, u32[]{:S(2)}, u32[]{:S(2)}) collective-permute-start(bf16[256,512]{1,0:T(8,128)(2,1)S(1)} %get-tuple-element.37), channel_id=1, source_target_pairs={{0,7},{1,0},{2,1},{3,2},{4,3},{5,4},{6,5},{7,6},{8,15},{9,8},{10,9... | collective-permute-start | bytes 786440 | tf_op jit(solution)/shard_map/ppermute | solution.py:41
  125.3 24.0 %collective-permute-start.16 = (bf16[256,512]{1,0:T(8,128)(2,1)}, bf16[256,512]{1,0:T(8,128)(2,1)S(1)}, u32[]{:S(2)}, u32[]{:S(2)}) collective-permute-start(bf16[256,512]{1,0:T(8,128)(2,1)} %get-tuple-element.39), channel_id=1, source_target_pairs={{0,1},{1,2},{2,3},{3,4},{4,5},{5,6},{6,7},{7,0},{8,9},{9,10},{10,1... | collective-permute-start | bytes 786440 | tf_op jit(solution)/shard_map/ppermute | solution.py:41
  126.0 20.3 %all-to-all-start.3 = ((bf16[16,16,256]{2,1,0:T(8,128)(2,1)}), bf16[16,16,256]{2,1,0:T(8,128)(2,1)S(1)}, u32[]{:S(2)}, u32[]{:S(2)}) async-start(bf16[16,16,256]{2,1,0:T(8,128)(2,1)} %broadcast_in_dim.125), calls=%async_computation.3 | async-start | bytes 262144 | tf_op jit(solution)/shard_map/all_to_all | solution.py:254
  138.5 10.9 %collective-permute-start.17 = (bf16[256,512]{1,0:T(8,128)(2,1)S(1)}, bf16[256,512]{1,0:T(8,128)(2,1)S(1)}, u32[]{:S(2)}, u32[]{:S(2)}) collective-permute-start(bf16[256,512]{1,0:T(8,128)(2,1)S(1)} %slice.87), channel_id=1, source_target_pairs={{0,8},{8,0},{16,24},{24,16},{32,40},{40,32},{48,56},{56,48},{64,72... | collective-permute-start | bytes 786440 | tf_op jit(solution)/shard_map/ppermute | solution.py:37
  139.0 10.5 %collective-permute-start.18 = (bf16[256,512]{1,0:T(8,128)(2,1)S(1)}, bf16[256,512]{1,0:T(8,128)(2,1)S(1)}, u32[]{:S(2)}, u32[]{:S(2)}) collective-permute-start(bf16[256,512]{1,0:T(8,128)(2,1)S(1)} %get-tuple-element.38), channel_id=1, source_target_pairs={{0,15},{1,8},{2,9},{3,10},{4,11},{5,12},{6,13},{7,14},{8,7},{9,0},... | collective-permute-start | bytes 786440 | tf_op jit(solution)/shard_map/ppermute | solution.py:50
  139.4 10.0 %collective-permute-start.19 = (bf16[256,512]{1,0:T(8,128)(2,1)S(1)}, bf16[256,512]{1,0:T(8,128)(2,1)S(1)}, u32[]{:S(2)}, u32[]{:S(2)}) collective-permute-start(bf16[256,512]{1,0:T(8,128)(2,1)S(1)} %get-tuple-element.40), channel_id=1, source_target_pairs={{0,9},{1,10},{2,11},{3,12},{4,13},{5,14},{6,15},{7,8},{8,1},{9,2},... | collective-permute-start | bytes 786440 | tf_op jit(solution)/shard_map/ppermute | solution.py:50
  (11 other events, 122.0 us)

commit v3 on v2

--- a/solution.py
+++ b/solution.py
@@ -215,7 +215,7 @@
         nonlocal shr_buf
         src = (x + d) % chips
         p = jnp.dot(tok, w_both, preferred_element_type=f32).astype(bf16)
-        bufs[q] = lax.dynamic_update_slice(bufs[q], p[None], (src, 0, 0))
+        bufs[q] = lax.dynamic_update_slice(bufs[q], p[None], ((src - y) % slices, 0, 0))
         s = lax.dot_general(
             down_chip, tok, (((1,), (1,)), ((), ())), preferred_element_type=f32
         ).astype(bf16)
@@ -245,6 +245,7 @@
         in_specs=[SMEM, SMEM, VMEM],
         out_specs=VMEM,
         cost_estimate=pl.CostEstimate(flops=10**7, bytes_accessed=10**6, transcendentals=0),
+        compiler_params=pltpu.CompilerParams(vmem_limit_bytes=6 * 2**20),
     )
     shr = pick(table, c[None], shr_buf)
     shr, up_all = lax.optimization_barrier((shr, up_all))
@@ -259,6 +260,7 @@
         in_specs=[SMEM, VMEM, VMEM, SMEM],
         out_specs=VMEM,
         cost_estimate=pl.CostEstimate(flops=10**7, bytes_accessed=10**6, transcendentals=0),
+        compiler_params=pltpu.CompilerParams(vmem_limit_bytes=6 * 2**20),
     )
     extra = expand(table, shr, up_all, y[None])
 
@@ -266,13 +268,13 @@
     m = k // 2
 
     def mine(t, lo, size):
-        return lax.dynamic_slice(bufs[0], (t % slices, lo, 0), (1, size, CORES * cols))[0]
+        return bufs[0][t % slices, lo : lo + size]
 
     dn, up, ends = [], [], []
     for r in range(STREAMS):
-        dn.append(shift_slices(mine(y + half, r * k, m), slices, -1))
-        up.append(shift_slices(mine(y + half, r * k + m, m), slices, 1))
-    last = mine(y, 0, rows)
+        dn.append(shift_slices(mine(half, r * k, m), slices, -1))
+        up.append(shift_slices(mine(half, r * k + m, m), slices, 1))
+    last = mine(0, 0, rows)
     oth = swap_cores(last[:, cols:], chips)
     before = None
     for h in range(half - 1, 0, -1):
@@ -281,8 +283,8 @@
                 dn[r], up[r] = lax.optimization_barrier((dn[r], up[r]))
             else:
                 dn[r], up[r], before = lax.optimization_barrier((dn[r], up[r], before))
-            d = mine(y + slices - h, r * k, k).astype(f32)
-            u = mine(y + h, r * k, k).astype(f32)
+            d = mine(slices - h, r * k, k).astype(f32)
+            u = mine(h, r * k, k).astype(f32)
             if h == half - 1:
                 d = jnp.concatenate([d[:m] + dn[r].astype(f32), d[m:]], axis=0)
                 u = jnp.concatenate([u[:m], u[m:] + up[r].astype(f32)], axis=0)

time: 153 us -> 145 us (0.948)
  starting transfers between devices: 70.7 us -> 59.2 us
  blocking collectives: 0 us -> 11.3 us
  local copies, waits for them, and re-layouts: 14.5 us -> 11.4 us
  other arithmetic: 10.4 us -> 7.46 us
  Pallas kernels: 7.25 us -> 4.69 us
    all_to_all x0 -> x1, blocking collectives: none -> 11.3 us  [on_device(): shr = lax.all_to_all(shr, 'tensor', 0, 0, tiled=True)]
    ppermute x2, waiting for transfers between devices: 0.01 us -> 6.47 us  [shift_slices_swap(): return lax.ppermute(v, ('adapter', 'tensor'), pairs)]
    all_to_all x1, waiting for transfers between devices: 5.48 us -> 0.01 us  [on_device(): shr = lax.all_to_all(shr, 'adapter', 0, 0, tiled=True)]
    all_to_all x1 -> x0, starting transfers between devices: 5.31 us -> none  [on_device(): shr = lax.all_to_all(shr, 'tensor', 0, 0, tiled=True)]
    ppermute x8, starting transfers between devices: 14.3 us -> 9.87 us  [shift_chips(): return lax.ppermute(v, 'adapter', pairs)]
    unnamed x23 -> x13, local copies, waits for them, and re-layouts: 6.59 us -> 3.15 us
  transfers between devices with their start and end apart: 25 -> 24, of which waited for: 9 -> 11; matrix products, arithmetic and copies ran while one was open for 20% -> 21% of each run, Pallas kernels for 5% -> 3%
where the time goes in v3:
time: 145 us; the launch traced here: 144 us
  starting transfers between devices  59.2 us (41%)
  waiting for transfers between devices  34.9 us (24%)
  matrix products  14.4 us (10%)
  local copies, waits for them, and re-layouts  11.4 us (8%)
  blocking collectives  11.3 us (8%)
  other arithmetic  7.46 us (5%)
  Pallas kernels  4.69 us (3%)
    ppermute x3, starting transfers between devices, swap_cores(): lax.ppermute(v, 'adapter', [(i, i ^ 1) for i in range(chips * CORES)])  20.3 us
    ppermute x8, waiting for transfers between devices, shift_chips(): return lax.ppermute(v, 'adapter', pairs)  15 us
    all_to_all x1, blocking collectives, on_device(): shr = lax.all_to_all(shr, 'tensor', 0, 0, tiled=True)  11.3 us
    ppermute x8, waiting for transfers between devices, shift_slices(): lax.ppermute(v, 'tensor', [(y, (y + step) % slices) for y in range(slices)])  10.3 us
    all_to_all x1, starting transfers between devices, on_device(): shr = lax.all_to_all(shr, 'adapter', 0, 0, tiled=True)  10.2 us
    ppermute x8, starting transfers between devices, shift_chips(): return lax.ppermute(v, 'adapter', pairs)  9.87 us
    ppermute x8, starting transfers between devices, shift_slices(): lax.ppermute(v, 'tensor', [(y, (y + step) % slices) for y in range(slices)])  9.67 us
    dot_general x8, matrix products, put(): p = jnp.dot(tok, w_both, preferred_element_type=f32).astype(bf16)  8.81 us
  transfers between devices with their start and end apart: 24, of which 11 were waited for; matrix products, arithmetic and copies ran while one was open for 21% of the time, Pallas kernels for 3%

profile of v3, /device:TPU:513, one launch (start us, length us, event | category | flops | bytes accessed | tf_op | source)
XLA Modules:
  0.0 143.8 jit_solution(16527777173948427171)
XLA Ops:
  0.0 2.2 %collective-permute-start.1 = (bf16[256,1024]{1,0:T(8,128)(2,1)}, bf16[256,1024]{1,0:T(8,128)(2,1)S(1)}, u32[]{:S(2)}, u32[]{:S(2)}) collective-permute-start(bf16[256,1024]{1,0:T(8,128)(2,1)} %param.7), channel_id=1, source_target_pairs={{0,16},{8,24},{16,32},{24,40},{32,48},{40,56},{48,64},{56,72},{64,... | collective-permute-start | bytes 1572872 | tf_op jit(solution)/shard_map/ppermute | solution.py:33
  2.2 2.2 %collective-permute-start.2 = (bf16[256,1024]{1,0:T(8,128)(2,1)}, bf16[256,1024]{1,0:T(8,128)(2,1)}, u32[]{:S(2)}, u32[]{:S(2)}) collective-permute-start(bf16[256,1024]{1,0:T(8,128)(2,1)} %param.7), channel_id=1, source_target_pairs={{0,112},{8,120},{16,0},{24,8},{32,16},{40,24},{48,32},{56,40},{64,... | collective-permute-start | bytes 1572872 | tf_op jit(solution)/shard_map/ppermute | solution.py:33
  4.4 19.3 %collective-permute-start = (bf16[1024,512]{1,0:T(8,128)(2,1)}, bf16[1024,512]{1,0:T(8,128)(2,1)S(1)}, u32[]{:S(2)}, u32[]{:S(2)}) collective-permute-start(bf16[1024,512]{1,0:T(8,128)(2,1)} %param.8), channel_id=1, source_target_pairs={{0,8},{8,0},{16,24},{24,16},{32,40},{40,32},{48,56},{56,48},{64,72... | collective-permute-start | bytes 3145736 | tf_op jit(solution)/shard_map/ppermute | solution.py:37
  24.2 3.2 %shard_map.73 = (s32[4,32]{1,0:T(4,128)}, bf16[64,1024]{1,0:T(8,128)(2,1)}, bf16[16,16,256]{2,1,0:T(8,128)(2,1)}) custom-call(s32[2]{0:T(128)} %pad_add_fusion.where, s32[32]{0:T(128)} %ids.1, s32[32]{0:T(128)} %live.1, s32[512]{0:T(512)} %index.1, bf16[32,16,1024]{2,1,0:T(8,128)(2,1)} %down.1, bf16[32,16,8192]{2,1,0:T(8,128)(2,1)} %up.1), custom_call_target="tpu_custom_call" | custom-call | flops 10000000 | bytes 1000000 | tf_op jit(solution)/shard_map/pallas_call | solution.py:182
  27.5 3.8 %all-to-all-start = ((bf16[16,16,256]{2,1,0:T(8,128)(2,1)}), bf16[16,16,256]{2,1,0:T(8,128)(2,1)S(1)}, u32[]{:S(2)}, u32[]{:S(2)}) async-start(bf16[16,16,256]{2,1,0:T(8,128)(2,1)} %get-tuple-element.24), calls=%async_computation | async-start | bytes 262144 | tf_op jit(solution)/shard_map/all_to_all | solution.py:207
  37.5 3.1 %all-to-all-done = bf16[16,16,256]{2,1,0:T(8,128)(2,1)S(1)} async-done(((bf16[16,16,256]{2,1,0:T(8,128)(2,1)}), bf16[16,16,256]{2,1,0:T(8,128)(2,1)S(1)}, u32[]{:S(2)}, u32[]{:S(2)}) %all-to-all-start) | async-done | bytes 131104 | tf_op jit(solution)/shard_map/all_to_all | solution.py:207
  42.3 3.6 %all-to-all-start.1 = ((bf16[8,4,16,256]{3,2,1,0:T(8,128)(2,1)}), bf16[8,4,16,256]{3,2,1,0:T(8,128)(2,1)S(1)}, u32[]{:S(2)}, u32[]{:S(2)}) async-start(bf16[8,4,16,256]{3,2,1,0:T(8,128)(2,1)} %broadcast_select_fusion), calls=%async_computation.1 | async-start | bytes 524288 | tf_op jit(solution)/shard_map/all_to_all | solution.py:209
  45.9 3.8 %collective-permute-done.3 = bf16[256,1024]{1,0:T(8,128)(2,1)} collective-permute-done((bf16[256,1024]{1,0:T(8,128)(2,1)S(1)}, bf16[256,1024]{1,0:T(8,128)(2,1)}, u32[]{:S(2)}, u32[]{:S(2)}) %collective-permute-start.3) | collective-permute-done | bytes 524320 | tf_op jit(solution)/shard_map/ppermute | solution.py:33
  53.3 2.3 %collective-permute-done.4 = bf16[256,1024]{1,0:T(8,128)(2,1)} collective-permute-done((bf16[256,1024]{1,0:T(8,128)(2,1)}, bf16[256,1024]{1,0:T(8,128)(2,1)}, u32[]{:S(2)}, u32[]{:S(2)}) %collective-permute-start.4) | collective-permute-done | bytes 524320 | tf_op jit(solution)/shard_map/ppermute | solution.py:33
  61.1 1.8 %fusion.11 = bf16[8,256,1024]{2,1,0:T(8,128)(2,1)S(1)} fusion(bf16[8,256,1024]{2,1,0:T(8,128)(2,1)S(1)} %fusion.9, s32[]{:T(128)S(6)} %select_n.166, bf16[256,1024]{1,0:T(8,128)(2,1)} %collective-permute-done.4, bf16[1024,1024]{1,0:T(8,128)(2,1)S(1)} %copy-done.3), kind=kOutput, calls=%fused_computation.20 | convolution fusion | flops 537133056 | bytes 3145732 | tf_op jit(solution)/shard_map/dot_general | solution.py:217
  63.7 5.2 %collective-permute-done.6 = bf16[256,1024]{1,0:T(8,128)(2,1)S(1)} collective-permute-done((bf16[256,1024]{1,0:T(8,128)(2,1)}, bf16[256,1024]{1,0:T(8,128)(2,1)S(1)}, u32[]{:S(2)}, u32[]{:S(2)}) %collective-permute-start.6) | collective-permute-done | bytes 524320 | tf_op jit(solution)/shard_map/ppermute | solution.py:33
  68.9 2.5 %collective-permute-start.8 = (bf16[128,1024]{1,0:T(8,128)(2,1)S(1)}, bf16[128,1024]{1,0:T(8,128)(2,1)S(1)}, u32[]{:S(2)}, u32[]{:S(2)}) collective-permute-start(bf16[128,1024]{1,0:T(8,128)(2,1)S(1)} %slice.117), channel_id=1, source_target_pairs={{0,112},{8,120},{16,0},{24,8},{32,16},{40,24},{48,32},{56,40},{64,... | collective-permute-start | bytes 786440 | tf_op jit(solution)/shard_map/ppermute | solution.py:33
  72.9 2.9 %collective-permute-done.8 = bf16[128,1024]{1,0:T(8,128)(2,1)S(1)} collective-permute-done((bf16[128,1024]{1,0:T(8,128)(2,1)S(1)}, bf16[128,1024]{1,0:T(8,128)(2,1)S(1)}, u32[]{:S(2)}, u32[]{:S(2)}) %collective-permute-start.8) | collective-permute-done | bytes 262176 | tf_op jit(solution)/shard_map/ppermute | solution.py:33
  76.8 2.6 %collective-permute-start.9 = (bf16[128,1024]{1,0:T(8,128)(2,1)S(1)}, bf16[128,1024]{1,0:T(8,128)(2,1)S(1)}, u32[]{:S(2)}, u32[]{:S(2)}) collective-permute-start(bf16[128,1024]{1,0:T(8,128)(2,1)S(1)} %get-tuple-element.34), channel_id=1, source_target_pairs={{0,7},{1,0},{2,1},{3,2},{4,3},{5,4},{6,5},{7,6},{8,15},{9,8},{10,9... | collective-permute-start | bytes 786440 | tf_op jit(solution)/shard_map/ppermute | solution.py:41
  81.1 2.6 %collective-permute-done.10 = bf16[128,1024]{1,0:T(8,128)(2,1)S(1)} collective-permute-done((bf16[128,1024]{1,0:T(8,128)(2,1)S(1)}, bf16[128,1024]{1,0:T(8,128)(2,1)S(1)}, u32[]{:S(2)}, u32[]{:S(2)}) %collective-permute-start.10) | collective-permute-done | bytes 262176 | tf_op jit(solution)/shard_map/ppermute | solution.py:41
  84.2 2.7 %collective-permute-start.11 = (bf16[256,1024]{1,0:T(8,128)(2,1)S(1)}, bf16[256,1024]{1,0:T(8,128)(2,1)S(1)}, u32[]{:S(2)}, u32[]{:S(2)}) collective-permute-start(bf16[256,1024]{1,0:T(8,128)(2,1)S(1)} %pad_maximum_fusion), channel_id=1, source_target_pairs={{0,7},{1,0},{2,1},{3,2},{4,3},{5,4},{6,5},{7,6},{8,15},{9,8},{10,9... | collective-permute-start | bytes 1572872 | tf_op jit(solution)/shard_map/ppermute | solution.py:41
  89.9 5.8 %collective-permute-done.12 = bf16[256,1024]{1,0:T(8,128)(2,1)S(1)} collective-permute-done((bf16[256,1024]{1,0:T(8,128)(2,1)S(1)}, bf16[256,1024]{1,0:T(8,128)(2,1)S(1)}, u32[]{:S(2)}, u32[]{:S(2)}) %collective-permute-start.12) | collective-permute-done | bytes 524320 | tf_op jit(solution)/shard_map/ppermute | solution.py:41
  97.0 2.5 %collective-permute-start.13 = (bf16[256,1024]{1,0:T(8,128)(2,1)}, bf16[256,1024]{1,0:T(8,128)(2,1)S(1)}, u32[]{:S(2)}, u32[]{:S(2)}) collective-permute-start(bf16[256,1024]{1,0:T(8,128)(2,1)} %get-tuple-element.30), channel_id=1, source_target_pairs={{0,7},{1,0},{2,1},{3,2},{4,3},{5,4},{6,5},{7,6},{8,15},{9,8},{10,9... | collective-permute-start | bytes 1572872 | tf_op jit(solution)/shard_map/ppermute | solution.py:41
  100.8 11.3 %all_to_all.20 = bf16[8,16,256]{2,1,0:T(8,128)(2,1)S(1)} all-to-all(bf16[8,16,256]{2,1,0:T(8,128)(2,1)S(1)} %pick.1), channel_id=1, replica_groups=mesh['groups'=2,'adapter'=16,'tensor'=8] {'tensor'}, dimensions={0} | all-to-all | bytes 131072 | tf_op jit(solution)/shard_map/all_to_all | solution.py:252
  112.8 10.2 %all-to-all-start.3 = ((bf16[16,16,256]{2,1,0:T(8,128)(2,1)}), bf16[16,16,256]{2,1,0:T(8,128)(2,1)S(1)}, u32[]{:S(2)}, u32[]{:S(2)}) async-start(bf16[16,16,256]{2,1,0:T(8,128)(2,1)} %broadcast_in_dim.125), calls=%async_computation.3 | async-start | bytes 262144 | tf_op jit(solution)/shard_map/all_to_all | solution.py:255
  123.1 1.8 %fusion.35 = (bf16[256,1024]{1,0:T(8,128)(2,1)S(1)}, bf16[256,1024]{1,0:T(8,128)(2,1)S(1)}) fusion(bf16[256,1024]{1,0:T(8,128)(2,1)S(1)} %collective-permute-done.13, bf16[8,256,1024]{2,1,0:T(8,128)(2,1)} %copy-done.1, bf16[256,1024]{1,0:T(8,128)(2,1)} %collective-permute-done.14), kind=kLoop, calls=%fused_computation.56 | loop fusion | flops 2097152 | bytes 3145728 | tf_op jit(solution)/shard_map/convert_element_type | solution.py:294
  133.3 1.9 %collective-permute-done.16 = bf16[256,512]{1,0:T(8,128)(2,1)S(1)} collective-permute-done((bf16[256,512]{1,0:T(8,128)(2,1)}, bf16[256,512]{1,0:T(8,128)(2,1)S(1)}, u32[]{:S(2)}, u32[]{:S(2)}) %collective-permute-start.16) | collective-permute-done | bytes 262176 | tf_op jit(solution)/shard_map/ppermute | solution.py:41
  135.3 4.3 %collective-permute-done.18 = bf16[256,512]{1,0:T(8,128)(2,1)S(1)} collective-permute-done((bf16[256,512]{1,0:T(8,128)(2,1)}, bf16[256,512]{1,0:T(8,128)(2,1)S(1)}, u32[]{:S(2)}, u32[]{:S(2)}) %collective-permute-start.18) | collective-permute-done | bytes 262176 | tf_op jit(solution)/shard_map/ppermute | solution.py:50
  139.6 2.1 %collective-permute-done.19 = bf16[256,512]{1,0:T(8,128)(2,1)} collective-permute-done((bf16[256,512]{1,0:T(8,128)(2,1)}, bf16[256,512]{1,0:T(8,128)(2,1)}, u32[]{:S(2)}, u32[]{:S(2)}) %collective-permute-start.19) | collective-permute-done | bytes 262176 | tf_op jit(solution)/shard_map/ppermute | solution.py:50
  (90 shorter events, 39.4 us)
Async XLA Ops:
  0.0 34.9 %collective-permute-start.1 = (bf16[256,1024]{1,0:T(8,128)(2,1)}, bf16[256,1024]{1,0:T(8,128)(2,1)S(1)}, u32[]{:S(2)}, u32[]{:S(2)}) collective-permute-start(bf16[256,1024]{1,0:T(8,128)(2,1)} %param.7), channel_id=1, source_target_pairs={{0,16},{8,24},{16,32},{24,40},{32,48},{40,56},{48,64},{56,72},{64,... | collective-permute-start | bytes 1572872 | tf_op jit(solution)/shard_map/ppermute | solution.py:33
  2.2 39.1 %collective-permute-start.2 = (bf16[256,1024]{1,0:T(8,128)(2,1)}, bf16[256,1024]{1,0:T(8,128)(2,1)}, u32[]{:S(2)}, u32[]{:S(2)}) collective-permute-start(bf16[256,1024]{1,0:T(8,128)(2,1)} %param.7), channel_id=1, source_target_pairs={{0,112},{8,120},{16,0},{24,8},{32,16},{40,24},{48,32},{56,40},{64,... | collective-permute-start | bytes 1572872 | tf_op jit(solution)/shard_map/ppermute | solution.py:33
  4.4 45.5 %collective-permute-start = (bf16[1024,512]{1,0:T(8,128)(2,1)}, bf16[1024,512]{1,0:T(8,128)(2,1)S(1)}, u32[]{:S(2)}, u32[]{:S(2)}) collective-permute-start(bf16[1024,512]{1,0:T(8,128)(2,1)} %param.8), channel_id=1, source_target_pairs={{0,8},{8,0},{16,24},{24,16},{32,40},{40,32},{48,56},{56,48},{64,72... | collective-permute-start | bytes 3145736 | tf_op jit(solution)/shard_map/ppermute | solution.py:37
  27.4 8.9 %collective-permute-start.20 = (bf16[64,1024]{1,0:T(8,128)(2,1)}, bf16[64,1024]{1,0:T(8,128)(2,1)}, u32[]{:S(2)}, u32[]{:S(2)}) collective-permute-start(bf16[64,1024]{1,0:T(8,128)(2,1)} %get-tuple-element.23), channel_id=1, source_target_pairs={{0,8},{8,0},{16,24},{24,16},{32,40},{40,32},{48,56},{56,48},{64,72... | collective-permute-start | bytes 393224 | tf_op jit(solution)/shard_map/ppermute | solution.py:37
  27.5 13.1 %all-to-all-start = ((bf16[16,16,256]{2,1,0:T(8,128)(2,1)}), bf16[16,16,256]{2,1,0:T(8,128)(2,1)S(1)}, u32[]{:S(2)}, u32[]{:S(2)}) async-start(bf16[16,16,256]{2,1,0:T(8,128)(2,1)} %get-tuple-element.24), calls=%async_computation | async-start | bytes 262144 | tf_op jit(solution)/shard_map/all_to_all | solution.py:207
  34.9 14.9 %collective-permute-start.3 = (bf16[256,1024]{1,0:T(8,128)(2,1)S(1)}, bf16[256,1024]{1,0:T(8,128)(2,1)}, u32[]{:S(2)}, u32[]{:S(2)}) collective-permute-start(bf16[256,1024]{1,0:T(8,128)(2,1)S(1)} %collective-permute-done.1), channel_id=1, source_target_pairs={{0,16},{8,24},{16,32},{24,40},{32,48},{40,56},{48,64},{56,72},{64,... | collective-permute-start | bytes 1572872 | tf_op jit(solution)/shard_map/ppermute | solution.py:33
  41.3 14.4 %collective-permute-start.4 = (bf16[256,1024]{1,0:T(8,128)(2,1)}, bf16[256,1024]{1,0:T(8,128)(2,1)}, u32[]{:S(2)}, u32[]{:S(2)}) collective-permute-start(bf16[256,1024]{1,0:T(8,128)(2,1)} %collective-permute-done.2), channel_id=1, source_target_pairs={{0,112},{8,120},{16,0},{24,8},{32,16},{40,24},{48,32},{56,40},{64,... | collective-permute-start | bytes 1572872 | tf_op jit(solution)/shard_map/ppermute | solution.py:33
  42.3 58.5 %all-to-all-start.1 = ((bf16[8,4,16,256]{3,2,1,0:T(8,128)(2,1)}), bf16[8,4,16,256]{3,2,1,0:T(8,128)(2,1)S(1)}, u32[]{:S(2)}, u32[]{:S(2)}) async-start(bf16[8,4,16,256]{3,2,1,0:T(8,128)(2,1)} %broadcast_select_fusion), calls=%async_computation.1 | async-start | bytes 524288 | tf_op jit(solution)/shard_map/all_to_all | solution.py:209
  49.8 13.7 %collective-permute-start.5 = (bf16[256,1024]{1,0:T(8,128)(2,1)}, bf16[256,1024]{1,0:T(8,128)(2,1)S(1)}, u32[]{:S(2)}, u32[]{:S(2)}) collective-permute-start(bf16[256,1024]{1,0:T(8,128)(2,1)} %collective-permute-done.3), channel_id=1, source_target_pairs={{0,16},{8,24},{16,32},{24,40},{32,48},{40,56},{48,64},{56,72},{64,... | collective-permute-start | bytes 1572872 | tf_op jit(solution)/shard_map/ppermute | solution.py:33
  55.6 13.3 %collective-permute-start.6 = (bf16[256,1024]{1,0:T(8,128)(2,1)}, bf16[256,1024]{1,0:T(8,128)(2,1)S(1)}, u32[]{:S(2)}, u32[]{:S(2)}) collective-permute-start(bf16[256,1024]{1,0:T(8,128)(2,1)} %collective-permute-done.4), channel_id=1, source_target_pairs={{0,112},{8,120},{16,0},{24,8},{32,16},{40,24},{48,32},{56,40},{64,... | collective-permute-start | bytes 1572872 | tf_op jit(solution)/shard_map/ppermute | solution.py:33
  63.5 9.3 %collective-permute-start.7 = (bf16[128,1024]{1,0:T(8,128)(2,1)S(1)}, bf16[128,1024]{1,0:T(8,128)(2,1)S(1)}, u32[]{:S(2)}, u32[]{:S(2)}) collective-permute-start(bf16[128,1024]{1,0:T(8,128)(2,1)S(1)} %slice.116), channel_id=1, source_target_pairs={{0,16},{8,24},{16,32},{24,40},{32,48},{40,56},{48,64},{56,72},{64,... | collective-permute-start | bytes 786440 | tf_op jit(solution)/shard_map/ppermute | solution.py:33
  68.9 6.9 %collective-permute-start.8 = (bf16[128,1024]{1,0:T(8,128)(2,1)S(1)}, bf16[128,1024]{1,0:T(8,128)(2,1)S(1)}, u32[]{:S(2)}, u32[]{:S(2)}) collective-permute-start(bf16[128,1024]{1,0:T(8,128)(2,1)S(1)} %slice.117), channel_id=1, source_target_pairs={{0,112},{8,120},{16,0},{24,8},{32,16},{40,24},{48,32},{56,40},{64,... | collective-permute-start | bytes 786440 | tf_op jit(solution)/shard_map/ppermute | solution.py:33
  76.7 7.0 %collective-permute-start.10 = (bf16[128,1024]{1,0:T(8,128)(2,1)S(1)}, bf16[128,1024]{1,0:T(8,128)(2,1)S(1)}, u32[]{:S(2)}, u32[]{:S(2)}) collective-permute-start(bf16[128,1024]{1,0:T(8,128)(2,1)S(1)} %get-tuple-element.33), channel_id=1, source_target_pairs={{0,1},{1,2},{2,3},{3,4},{4,5},{5,6},{6,7},{7,0},{8,9},{9,10},{10,1... | collective-permute-start | bytes 786440 | tf_op jit(solution)/shard_map/ppermute | solution.py:41
  76.8 6.9 %collective-permute-start.9 = (bf16[128,1024]{1,0:T(8,128)(2,1)S(1)}, bf16[128,1024]{1,0:T(8,128)(2,1)S(1)}, u32[]{:S(2)}, u32[]{:S(2)}) collective-permute-start(bf16[128,1024]{1,0:T(8,128)(2,1)S(1)} %get-tuple-element.34), channel_id=1, source_target_pairs={{0,7},{1,0},{2,1},{3,2},{4,3},{5,4},{6,5},{7,6},{8,15},{9,8},{10,9... | collective-permute-start | bytes 786440 | tf_op jit(solution)/shard_map/ppermute | solution.py:41
  84.0 11.8 %collective-permute-start.12 = (bf16[256,1024]{1,0:T(8,128)(2,1)S(1)}, bf16[256,1024]{1,0:T(8,128)(2,1)S(1)}, u32[]{:S(2)}, u32[]{:S(2)}) collective-permute-start(bf16[256,1024]{1,0:T(8,128)(2,1)S(1)} %pad_maximum_fusion.1), channel_id=1, source_target_pairs={{0,1},{1,2},{2,3},{3,4},{4,5},{5,6},{6,7},{7,0},{8,9},{9,10},{10,1... | collective-permute-start | bytes 1572872 | tf_op jit(solution)/shard_map/ppermute | solution.py:41
  84.2 11.6 %collective-permute-start.11 = (bf16[256,1024]{1,0:T(8,128)(2,1)S(1)}, bf16[256,1024]{1,0:T(8,128)(2,1)S(1)}, u32[]{:S(2)}, u32[]{:S(2)}) collective-permute-start(bf16[256,1024]{1,0:T(8,128)(2,1)S(1)} %pad_maximum_fusion), channel_id=1, source_target_pairs={{0,7},{1,0},{2,1},{3,2},{4,3},{5,4},{6,5},{7,6},{8,15},{9,8},{10,9... | collective-permute-start | bytes 1572872 | tf_op jit(solution)/shard_map/ppermute | solution.py:41
  97.0 26.1 %collective-permute-start.13 = (bf16[256,1024]{1,0:T(8,128)(2,1)}, bf16[256,1024]{1,0:T(8,128)(2,1)S(1)}, u32[]{:S(2)}, u32[]{:S(2)}) collective-permute-start(bf16[256,1024]{1,0:T(8,128)(2,1)} %get-tuple-element.30), channel_id=1, source_target_pairs={{0,7},{1,0},{2,1},{3,2},{4,3},{5,4},{6,5},{7,6},{8,15},{9,8},{10,9... | collective-permute-start | bytes 1572872 | tf_op jit(solution)/shard_map/ppermute | solution.py:41
  99.5 23.5 %collective-permute-start.14 = (bf16[256,1024]{1,0:T(8,128)(2,1)S(1)}, bf16[256,1024]{1,0:T(8,128)(2,1)}, u32[]{:S(2)}, u32[]{:S(2)}) collective-permute-start(bf16[256,1024]{1,0:T(8,128)(2,1)S(1)} %get-tuple-element.29), channel_id=1, source_target_pairs={{0,1},{1,2},{2,3},{3,4},{4,5},{5,6},{6,7},{7,0},{8,9},{9,10},{10,1... | collective-permute-start | bytes 1572872 | tf_op jit(solution)/shard_map/ppermute | solution.py:41
  112.8 19.6 %all-to-all-start.3 = ((bf16[16,16,256]{2,1,0:T(8,128)(2,1)}), bf16[16,16,256]{2,1,0:T(8,128)(2,1)S(1)}, u32[]{:S(2)}, u32[]{:S(2)}) async-start(bf16[16,16,256]{2,1,0:T(8,128)(2,1)} %broadcast_in_dim.125), calls=%async_computation.3 | async-start | bytes 262144 | tf_op jit(solution)/shard_map/all_to_all | solution.py:255
  125.6 7.7 %collective-permute-start.15 = (bf16[256,512]{1,0:T(8,128)(2,1)S(1)}, bf16[256,512]{1,0:T(8,128)(2,1)S(1)}, u32[]{:S(2)}, u32[]{:S(2)}) collective-permute-start(bf16[256,512]{1,0:T(8,128)(2,1)S(1)} %get-tuple-element.37), channel_id=1, source_target_pairs={{0,7},{1,0},{2,1},{3,2},{4,3},{5,4},{6,5},{7,6},{8,15},{9,8},{10,9... | collective-permute-start | bytes 786440 | tf_op jit(solution)/shard_map/ppermute | solution.py:41
  126.4 8.8 %collective-permute-start.16 = (bf16[256,512]{1,0:T(8,128)(2,1)}, bf16[256,512]{1,0:T(8,128)(2,1)S(1)}, u32[]{:S(2)}, u32[]{:S(2)}) collective-permute-start(bf16[256,512]{1,0:T(8,128)(2,1)} %get-tuple-element.39), channel_id=1, source_target_pairs={{0,1},{1,2},{2,3},{3,4},{4,5},{5,6},{6,7},{7,0},{8,9},{9,10},{10,1... | collective-permute-start | bytes 786440 | tf_op jit(solution)/shard_map/ppermute | solution.py:41
  129.7 5.6 %collective-permute-start.17 = (bf16[256,512]{1,0:T(8,128)(2,1)}, bf16[256,512]{1,0:T(8,128)(2,1)S(1)}, u32[]{:S(2)}, u32[]{:S(2)}) collective-permute-start(bf16[256,512]{1,0:T(8,128)(2,1)} %slice.132), channel_id=1, source_target_pairs={{0,8},{8,0},{16,24},{24,16},{32,40},{40,32},{48,56},{56,48},{64,72... | collective-permute-start | bytes 786440 | tf_op jit(solution)/shard_map/ppermute | solution.py:37
  130.5 9.1 %collective-permute-start.18 = (bf16[256,512]{1,0:T(8,128)(2,1)}, bf16[256,512]{1,0:T(8,128)(2,1)S(1)}, u32[]{:S(2)}, u32[]{:S(2)}) collective-permute-start(bf16[256,512]{1,0:T(8,128)(2,1)} %get-tuple-element.38), channel_id=1, source_target_pairs={{0,15},{1,8},{2,9},{3,10},{4,11},{5,12},{6,13},{7,14},{8,7},{9,0},... | collective-permute-start | bytes 786440 | tf_op jit(solution)/shard_map/ppermute | solution.py:50
  131.6 10.2 %collective-permute-start.19 = (bf16[256,512]{1,0:T(8,128)(2,1)}, bf16[256,512]{1,0:T(8,128)(2,1)}, u32[]{:S(2)}, u32[]{:S(2)}) collective-permute-start(bf16[256,512]{1,0:T(8,128)(2,1)} %get-tuple-element.40), channel_id=1, source_target_pairs={{0,9},{1,10},{2,11},{3,12},{4,13},{5,14},{6,15},{7,8},{8,1},{9,2},... | collective-permute-start | bytes 786440 | tf_op jit(solution)/shard_map/ppermute | solution.py:50
  (5 other events, 59.4 us)

commit v4 on v3

--- a/solution.py
+++ b/solution.py
@@ -4,6 +4,7 @@
 import jax.numpy as jnp
 from jax import lax
 from jax.experimental import pallas as pl
+from jax.experimental.layout import Layout, with_layout_constraint
 from jax.experimental.pallas import tpu as pltpu
 from jax.sharding import PartitionSpec as P
 
@@ -215,6 +216,7 @@
         nonlocal shr_buf
         src = (x + d) % chips
         p = jnp.dot(tok, w_both, preferred_element_type=f32).astype(bf16)
+        p = with_layout_constraint(p, Layout((0, 1)))
         bufs[q] = lax.dynamic_update_slice(bufs[q], p[None], ((src - y) % slices, 0, 0))
         s = lax.dot_general(
             down_chip, tok, (((1,), (1,)), ((), ())), preferred_element_type=f32
@@ -270,38 +272,35 @@
     def mine(t, lo, size):
         return bufs[0][t % slices, lo : lo + size]
 
-    dn, up, ends = [], [], []
-    for r in range(STREAMS):
-        dn.append(shift_slices(mine(half, r * k, m), slices, -1))
-        up.append(shift_slices(mine(half, r * k + m, m), slices, 1))
+    h = half - 1
+    dn = shift_slices(mine(half, 0, m), slices, -1)
+    up = shift_slices(mine(half, m, m), slices, 1)
+    dn_b = shift_slices(mine(slices - h, m, m), slices, -1)
+    up_b = shift_slices(mine(h, 0, m), slices, 1)
     last = mine(0, 0, rows)
     oth = swap_cores(last[:, cols:], chips)
-    before = None
-    for h in range(half - 1, 0, -1):
-        for r in range(STREAMS):
-            if before is None:
-                dn[r], up[r] = lax.optimization_barrier((dn[r], up[r]))
-            else:
-                dn[r], up[r], before = lax.optimization_barrier((dn[r], up[r], before))
-            d = mine(slices - h, r * k, k).astype(f32)
-            u = mine(h, r * k, k).astype(f32)
-            if h == half - 1:
-                d = jnp.concatenate([d[:m] + dn[r].astype(f32), d[m:]], axis=0)
-                u = jnp.concatenate([u[:m], u[m:] + up[r].astype(f32)], axis=0)
-            else:
-                d = d + dn[r].astype(f32)
-                u = u + up[r].astype(f32)
-            d, u = d.astype(bf16), u.astype(bf16)
-            if h == 1:
-                d, dx = d[:, :cols], d[:, cols:]
-                u, ux = u[:, :cols], u[:, cols:]
-            before = d
-            dn[r] = shift_slices(d, slices, -1)
-            up[r] = shift_slices(u, slices, 1)
-            if h == 1:
-                dx = shift_slices_swap(dx, owners, slices, -1)
-                ux = shift_slices_swap(ux, owners, slices, 1)
-                ends += [dn[r], up[r], dx, ux]
+    dn, up = lax.optimization_barrier((dn, up))
+    d = (mine(slices - h, 0, m).astype(f32) + dn.astype(f32)).astype(bf16)
+    u = (mine(h, m, m).astype(f32) + up.astype(f32)).astype(bf16)
+    dn = shift_slices(d, slices, -1)
+    up = shift_slices(u, slices, 1)
+    dn, up, dn_b, up_b = lax.optimization_barrier((dn, up, dn_b, up_b))
+    dn = jnp.concatenate([dn, dn_b], axis=0)
+    up = jnp.concatenate([up_b, up], axis=0)
+    for h in range(half - 2, 0, -1):
+        if h < half - 2:
+            dn, up = lax.optimization_barrier((dn, up))
+        d = (mine(slices - h, 0, rows).astype(f32) + dn.astype(f32)).astype(bf16)
+        u = (mine(h, 0, rows).astype(f32) + up.astype(f32)).astype(bf16)
+        if h > 1:
+            dn = shift_slices(d, slices, -1)
+            up = shift_slices(u, slices, 1)
+        else:
+            dn = shift_slices(d[:, :cols], slices, -1)
+            up = shift_slices(u[:, :cols], slices, 1)
+            dx = shift_slices_swap(d[:, cols:], owners, slices, -1)
+            ux = shift_slices_swap(u[:, cols:], owners, slices, 1)
+    ends = [dn, up, dx, ux]
     out = []
     order = lax.broadcasted_iota(i32, (CORES, k, cols), 0)
     extra = extra.reshape(CORES, rows, cols)

time: 145 us -> 150 us (1.034)
  waiting for transfers between devices: 34.9 us -> 38.9 us
  starting transfers between devices: 59.2 us -> 61.8 us
  matrix products: 14.4 us -> 12.3 us
  blocking collectives: 11.3 us -> 12.9 us
    ppermute x8, waiting for transfers between devices: 15 us -> 18.2 us  [shift_chips(): return lax.ppermute(v, 'adapter', pairs)]
    all_to_all x1, blocking collectives: 11.3 us -> 12.9 us  [on_device(): shr = lax.all_to_all(shr, 'tensor', 0, 0, tiled=True)]
    ppermute x8 -> x10, waiting for transfers between devices: 10.3 us -> 11.4 us  [shift_slices(): lax.ppermute(v, 'tensor', [(y, (y + step) % slices) for y in range(slices)])]
    ppermute x8 -> x10, starting transfers between devices: 9.67 us -> 10.3 us  [shift_slices(): lax.ppermute(v, 'tensor', [(y, (y + step) % slices) for y in range(slices)])]
    convert_element_type x2 -> x3, other arithmetic: 2.96 us -> 3.17 us  [the longest x1 1.76 us: on_device(): d = (mine(slices - h, 0, rows).astype(f32) + dn.astype(f32)).astype(bf16)]
  transfers between devices with their start and end apart: 24 -> 26, of which waited for: 11 -> 12; matrix products, arithmetic and copies ran while one was open for 21% -> 19% of each run, Pallas kernels for 3% -> 3%
where the time goes in v4:
time: 150 us; the launch traced here: 149 us
  starting transfers between devices  61.8 us (41%)
  waiting for transfers between devices  38.9 us (26%)
  blocking collectives  12.9 us (9%)
  matrix products  12.3 us (8%)
  local copies, waits for them, and re-layouts  11.5 us (8%)
  other arithmetic  6.52 us (4%)
  Pallas kernels  4.69 us (3%)
    ppermute x3, starting transfers between devices, swap_cores(): lax.ppermute(v, 'adapter', [(i, i ^ 1) for i in range(chips * CORES)])  20.3 us
    ppermute x8, waiting for transfers between devices, shift_chips(): return lax.ppermute(v, 'adapter', pairs)  18.2 us
    all_to_all x1, blocking collectives, on_device(): shr = lax.all_to_all(shr, 'tensor', 0, 0, tiled=True)  12.9 us
    ppermute x10, waiting for transfers between devices, shift_slices(): lax.ppermute(v, 'tensor', [(y, (y + step) % slices) for y in range(slices)])  11.4 us
    all_to_all x1, starting transfers between devices, on_device(): shr = lax.all_to_all(shr, 'adapter', 0, 0, tiled=True)  11.3 us
    ppermute x8, starting transfers between devices, shift_chips(): return lax.ppermute(v, 'adapter', pairs)  10.8 us
    ppermute x10, starting transfers between devices, shift_slices(): lax.ppermute(v, 'tensor', [(y, (y + step) % slices) for y in range(slices)])  10.3 us
    dot_general x8, matrix products, put(): p = jnp.dot(tok, w_both, preferred_element_type=f32).astype(bf16)  7.77 us
  transfers between devices with their start and end apart: 26, of which 12 were waited for; matrix products, arithmetic and copies ran while one was open for 19% of the time, Pallas kernels for 3%

profile of v4, /device:TPU:513, one launch (start us, length us, event | category | flops | bytes accessed | tf_op | source)
XLA Modules:
  0.0 149.0 jit_solution(2361964297353371054)
XLA Ops:
  0.0 2.2 %collective-permute-start.1 = (bf16[256,1024]{1,0:T(8,128)(2,1)}, bf16[256,1024]{1,0:T(8,128)(2,1)}, u32[]{:S(2)}, u32[]{:S(2)}) collective-permute-start(bf16[256,1024]{1,0:T(8,128)(2,1)} %param.7), channel_id=1, source_target_pairs={{0,16},{8,24},{16,32},{24,40},{32,48},{40,56},{48,64},{56,72},{64,... | collective-permute-start | bytes 1572872 | tf_op jit(solution)/shard_map/ppermute | solution.py:34
  2.2 2.2 %collective-permute-start.2 = (bf16[256,1024]{1,0:T(8,128)(2,1)}, bf16[256,1024]{1,0:T(8,128)(2,1)S(1)}, u32[]{:S(2)}, u32[]{:S(2)}) collective-permute-start(bf16[256,1024]{1,0:T(8,128)(2,1)} %param.7), channel_id=1, source_target_pairs={{0,112},{8,120},{16,0},{24,8},{32,16},{40,24},{48,32},{56,40},{64,... | collective-permute-start | bytes 1572872 | tf_op jit(solution)/shard_map/ppermute | solution.py:34
  4.4 19.3 %collective-permute-start = (bf16[1024,512]{1,0:T(8,128)(2,1)}, bf16[1024,512]{1,0:T(8,128)(2,1)S(1)}, u32[]{:S(2)}, u32[]{:S(2)}) collective-permute-start(bf16[1024,512]{1,0:T(8,128)(2,1)} %param.8), channel_id=1, source_target_pairs={{0,8},{8,0},{16,24},{24,16},{32,40},{40,32},{48,56},{56,48},{64,72... | collective-permute-start | bytes 3145736 | tf_op jit(solution)/shard_map/ppermute | solution.py:38
  24.3 3.2 %shard_map.73 = (s32[4,32]{1,0:T(4,128)}, bf16[64,1024]{1,0:T(8,128)(2,1)}, bf16[16,16,256]{2,1,0:T(8,128)(2,1)}) custom-call(s32[2]{0:T(128)} %pad_add_fusion.where, s32[32]{0:T(128)} %ids.1, s32[32]{0:T(128)} %live.1, s32[512]{0:T(512)} %index.1, bf16[32,16,1024]{2,1,0:T(8,128)(2,1)} %down.1, bf16[32,16,8192]{2,1,0:T(8,128)(2,1)} %up.1), custom_call_target="tpu_custom_call" | custom-call | flops 10000000 | bytes 1000000 | tf_op jit(solution)/shard_map/pallas_call | solution.py:183
  27.6 3.8 %all-to-all-start = ((bf16[16,16,256]{2,1,0:T(8,128)(2,1)}), bf16[16,16,256]{2,1,0:T(8,128)(2,1)S(1)}, u32[]{:S(2)}, u32[]{:S(2)}) async-start(bf16[16,16,256]{2,1,0:T(8,128)(2,1)} %get-tuple-element.28), calls=%async_computation | async-start | bytes 262144 | tf_op jit(solution)/shard_map/all_to_all | solution.py:208
  37.8 2.9 %all-to-all-done = bf16[16,16,256]{2,1,0:T(8,128)(2,1)S(1)} async-done(((bf16[16,16,256]{2,1,0:T(8,128)(2,1)}), bf16[16,16,256]{2,1,0:T(8,128)(2,1)S(1)}, u32[]{:S(2)}, u32[]{:S(2)}) %all-to-all-start) | async-done | bytes 131104 | tf_op jit(solution)/shard_map/all_to_all | solution.py:208
  42.0 3.6 %all-to-all-start.1 = ((bf16[8,4,16,256]{3,2,1,0:T(8,128)(2,1)}), bf16[8,4,16,256]{3,2,1,0:T(8,128)(2,1)S(1)}, u32[]{:S(2)}, u32[]{:S(2)}) async-start(bf16[8,4,16,256]{3,2,1,0:T(8,128)(2,1)} %broadcast_select_fusion), calls=%async_computation.1 | async-start | bytes 524288 | tf_op jit(solution)/shard_map/all_to_all | solution.py:210
  47.3 3.6 %collective-permute-done.3 = bf16[256,1024]{1,0:T(8,128)(2,1)} collective-permute-done((bf16[256,1024]{1,0:T(8,128)(2,1)}, bf16[256,1024]{1,0:T(8,128)(2,1)}, u32[]{:S(2)}, u32[]{:S(2)}) %collective-permute-start.3) | collective-permute-done | bytes 524320 | tf_op jit(solution)/shard_map/ppermute | solution.py:34
  54.3 5.3 %collective-permute-done.4 = bf16[256,1024]{1,0:T(8,128)(2,1)S(1)} collective-permute-done((bf16[256,1024]{1,0:T(8,128)(2,1)S(1)}, bf16[256,1024]{1,0:T(8,128)(2,1)S(1)}, u32[]{:S(2)}, u32[]{:S(2)}) %collective-permute-start.4) | collective-permute-done | bytes 524320 | tf_op jit(solution)/shard_map/ppermute | solution.py:34
  63.5 1.8 %fusion.9 = bf16[8,256,1024]{2,1,0:T(8,128)(2,1)S(1)} fusion(bf16[8,256,1024]{2,1,0:T(8,128)(2,1)S(1)} %fusion.7, s32[]{:T(128)S(6)} %select_n.163, bf16[256,1024]{1,0:T(8,128)(2,1)} %collective-permute-done.3, bf16[1024,1024]{1,0:T(8,128)(2,1)S(1)} %copy-done.3), kind=kOutput, calls=%fused_computation.18 | convolution fusion | flops 537133056 | bytes 3145732 | tf_op jit(solution)/shard_map/dot_general | solution.py:218
  66.2 6.4 %collective-permute-done.6 = bf16[256,1024]{1,0:T(8,128)(2,1)S(1)} collective-permute-done((bf16[256,1024]{1,0:T(8,128)(2,1)S(1)}, bf16[256,1024]{1,0:T(8,128)(2,1)S(1)}, u32[]{:S(2)}, u32[]{:S(2)}) %collective-permute-start.6) | collective-permute-done | bytes 524320 | tf_op jit(solution)/shard_map/ppermute | solution.py:34
  72.6 3.0 %collective-permute-start.8 = (bf16[128,1024]{1,0:T(8,128)(2,1)S(1)}, bf16[128,1024]{1,0:T(8,128)(2,1)S(1)}, u32[]{:S(2)}, u32[]{:S(2)}) collective-permute-start(bf16[128,1024]{1,0:T(8,128)(2,1)S(1)} %slice.83), channel_id=1, source_target_pairs={{0,112},{8,120},{16,0},{24,8},{32,16},{40,24},{48,32},{56,40},{64,... | collective-permute-start | bytes 786440 | tf_op jit(solution)/shard_map/ppermute | solution.py:34
  77.1 2.9 %collective-permute-done.8 = bf16[128,1024]{1,0:T(8,128)(2,1)S(1)} collective-permute-done((bf16[128,1024]{1,0:T(8,128)(2,1)S(1)}, bf16[128,1024]{1,0:T(8,128)(2,1)S(1)}, u32[]{:S(2)}, u32[]{:S(2)}) %collective-permute-start.8) | collective-permute-done | bytes 262176 | tf_op jit(solution)/shard_map/ppermute | solution.py:34
  81.5 2.2 %collective-permute-start.9 = (bf16[128,1024]{1,0:T(8,128)(2,1)S(1)}, bf16[128,1024]{1,0:T(8,128)(2,1)S(1)}, u32[]{:S(2)}, u32[]{:S(2)}) collective-permute-start(bf16[128,1024]{1,0:T(8,128)(2,1)S(1)} %get-tuple-element.38), channel_id=1, source_target_pairs={{0,7},{1,0},{2,1},{3,2},{4,3},{5,4},{6,5},{7,6},{8,15},{9,8},{10,9... | collective-permute-start | bytes 786440 | tf_op jit(solution)/shard_map/ppermute | solution.py:42
  88.2 2.2 %collective-permute-start.11 = (bf16[128,1024]{1,0:T(8,128)(2,1)S(1)}, bf16[128,1024]{1,0:T(8,128)(2,1)S(1)}, u32[]{:S(2)}, u32[]{:S(2)}) collective-permute-start(bf16[128,1024]{1,0:T(8,128)(2,1)S(1)} %get-tuple-element.40), channel_id=1, source_target_pairs={{0,7},{1,0},{2,1},{3,2},{4,3},{5,4},{6,5},{7,6},{8,15},{9,8},{10,9... | collective-permute-start | bytes 786440 | tf_op jit(solution)/shard_map/ppermute | solution.py:42
  91.1 2.7 %collective-permute-done.13 = bf16[128,1024]{1,0:T(8,128)(2,1)S(1)} collective-permute-done((bf16[128,1024]{1,0:T(8,128)(2,1)S(1)}, bf16[128,1024]{1,0:T(8,128)(2,1)S(1)}, u32[]{:S(2)}, u32[]{:S(2)}) %collective-permute-start.13) | collective-permute-done | bytes 262176 | tf_op jit(solution)/shard_map/ppermute | solution.py:42
  93.8 5.6 %collective-permute-done.11 = bf16[128,1024]{1,0:T(8,128)(2,1)S(1)} collective-permute-done((bf16[128,1024]{1,0:T(8,128)(2,1)S(1)}, bf16[128,1024]{1,0:T(8,128)(2,1)S(1)}, u32[]{:S(2)}, u32[]{:S(2)}) %collective-permute-start.11) | collective-permute-done | bytes 262176 | tf_op jit(solution)/shard_map/ppermute | solution.py:42
  100.7 2.2 %collective-permute-start.15 = (bf16[256,1024]{1,0:T(8,128)(2,1)}, bf16[256,1024]{1,0:T(8,128)(2,1)S(1)}, u32[]{:S(2)}, u32[]{:S(2)}) collective-permute-start(bf16[256,1024]{1,0:T(8,128)(2,1)} %get-tuple-element.34), channel_id=1, source_target_pairs={{0,7},{1,0},{2,1},{3,2},{4,3},{5,4},{6,5},{7,6},{8,15},{9,8},{10,9... | collective-permute-start | bytes 1572872 | tf_op jit(solution)/shard_map/ppermute | solution.py:42
  104.2 12.9 %all_to_all.20 = bf16[8,16,256]{2,1,0:T(8,128)(2,1)S(1)} all-to-all(bf16[8,16,256]{2,1,0:T(8,128)(2,1)S(1)} %pick.1), channel_id=1, replica_groups=mesh['groups'=2,'adapter'=16,'tensor'=8] {'tensor'}, dimensions={0} | all-to-all | bytes 131072 | tf_op jit(solution)/shard_map/all_to_all | solution.py:254
  117.7 11.3 %all-to-all-start.3 = ((bf16[16,16,256]{2,1,0:T(8,128)(2,1)}), bf16[16,16,256]{2,1,0:T(8,128)(2,1)S(1)}, u32[]{:S(2)}, u32[]{:S(2)}) async-start(bf16[16,16,256]{2,1,0:T(8,128)(2,1)} %broadcast_in_dim.125), calls=%async_computation.3 | async-start | bytes 262144 | tf_op jit(solution)/shard_map/all_to_all | solution.py:257
  129.0 1.8 %fusion.35 = (bf16[256,1024]{1,0:T(8,128)(2,1)S(1)}, bf16[256,1024]{1,0:T(8,128)(2,1)S(1)}) fusion(bf16[256,1024]{1,0:T(8,128)(2,1)S(1)} %collective-permute-done.15, bf16[8,256,1024]{2,1,0:T(8,128)(2,1)} %copy-done.1, bf16[256,1024]{1,0:T(8,128)(2,1)} %collective-permute-done.16), kind=kLoop, calls=%fused_computation.56 | loop fusion | flops 2097152 | bytes 3145728 | tf_op jit(solution)/shard_map/convert_element_type | solution.py:293
  139.4 1.9 %collective-permute-done.18 = bf16[256,512]{1,0:T(8,128)(2,1)S(1)} collective-permute-done((bf16[256,512]{1,0:T(8,128)(2,1)}, bf16[256,512]{1,0:T(8,128)(2,1)S(1)}, u32[]{:S(2)}, u32[]{:S(2)}) %collective-permute-start.18) | collective-permute-done | bytes 262176 | tf_op jit(solution)/shard_map/ppermute | solution.py:42
  141.5 4.3 %collective-permute-done.20 = bf16[256,512]{1,0:T(8,128)(2,1)S(1)} collective-permute-done((bf16[256,512]{1,0:T(8,128)(2,1)}, bf16[256,512]{1,0:T(8,128)(2,1)S(1)}, u32[]{:S(2)}, u32[]{:S(2)}) %collective-permute-start.20) | collective-permute-done | bytes 262176 | tf_op jit(solution)/shard_map/ppermute | solution.py:51
  145.8 2.0 %collective-permute-done.21 = bf16[256,512]{1,0:T(8,128)(2,1)S(1)} collective-permute-done((bf16[256,512]{1,0:T(8,128)(2,1)}, bf16[256,512]{1,0:T(8,128)(2,1)S(1)}, u32[]{:S(2)}, u32[]{:S(2)}) %collective-permute-start.21) | collective-permute-done | bytes 262176 | tf_op jit(solution)/shard_map/ppermute | solution.py:51
  (92 shorter events, 39.3 us)
Async XLA Ops:
  0.0 35.9 %collective-permute-start.1 = (bf16[256,1024]{1,0:T(8,128)(2,1)}, bf16[256,1024]{1,0:T(8,128)(2,1)}, u32[]{:S(2)}, u32[]{:S(2)}) collective-permute-start(bf16[256,1024]{1,0:T(8,128)(2,1)} %param.7), channel_id=1, source_target_pairs={{0,16},{8,24},{16,32},{24,40},{32,48},{40,56},{48,64},{56,72},{64,... | collective-permute-start | bytes 1572872 | tf_op jit(solution)/shard_map/ppermute | solution.py:34
  2.2 43.5 %collective-permute-start.2 = (bf16[256,1024]{1,0:T(8,128)(2,1)}, bf16[256,1024]{1,0:T(8,128)(2,1)S(1)}, u32[]{:S(2)}, u32[]{:S(2)}) collective-permute-start(bf16[256,1024]{1,0:T(8,128)(2,1)} %param.7), channel_id=1, source_target_pairs={{0,112},{8,120},{16,0},{24,8},{32,16},{40,24},{48,32},{56,40},{64,... | collective-permute-start | bytes 1572872 | tf_op jit(solution)/shard_map/ppermute | solution.py:34
  4.4 46.5 %collective-permute-start = (bf16[1024,512]{1,0:T(8,128)(2,1)}, bf16[1024,512]{1,0:T(8,128)(2,1)S(1)}, u32[]{:S(2)}, u32[]{:S(2)}) collective-permute-start(bf16[1024,512]{1,0:T(8,128)(2,1)} %param.8), channel_id=1, source_target_pairs={{0,8},{8,0},{16,24},{24,16},{32,40},{40,32},{48,56},{56,48},{64,72... | collective-permute-start | bytes 3145736 | tf_op jit(solution)/shard_map/ppermute | solution.py:38
  27.5 7.5 %collective-permute-start.22 = (bf16[64,1024]{1,0:T(8,128)(2,1)}, bf16[64,1024]{1,0:T(8,128)(2,1)}, u32[]{:S(2)}, u32[]{:S(2)}) collective-permute-start(bf16[64,1024]{1,0:T(8,128)(2,1)} %get-tuple-element.27), channel_id=1, source_target_pairs={{0,8},{8,0},{16,24},{24,16},{32,40},{40,32},{48,56},{56,48},{64,72... | collective-permute-start | bytes 393224 | tf_op jit(solution)/shard_map/ppermute | solution.py:38
  27.6 13.1 %all-to-all-start = ((bf16[16,16,256]{2,1,0:T(8,128)(2,1)}), bf16[16,16,256]{2,1,0:T(8,128)(2,1)S(1)}, u32[]{:S(2)}, u32[]{:S(2)}) async-start(bf16[16,16,256]{2,1,0:T(8,128)(2,1)} %get-tuple-element.28), calls=%async_computation | async-start | bytes 262144 | tf_op jit(solution)/shard_map/all_to_all | solution.py:208
  35.9 15.0 %collective-permute-start.3 = (bf16[256,1024]{1,0:T(8,128)(2,1)}, bf16[256,1024]{1,0:T(8,128)(2,1)}, u32[]{:S(2)}, u32[]{:S(2)}) collective-permute-start(bf16[256,1024]{1,0:T(8,128)(2,1)} %collective-permute-done.1), channel_id=1, source_target_pairs={{0,16},{8,24},{16,32},{24,40},{32,48},{40,56},{48,64},{56,72},{64,... | collective-permute-start | bytes 1572872 | tf_op jit(solution)/shard_map/ppermute | solution.py:34
  42.0 62.1 %all-to-all-start.1 = ((bf16[8,4,16,256]{3,2,1,0:T(8,128)(2,1)}), bf16[8,4,16,256]{3,2,1,0:T(8,128)(2,1)S(1)}, u32[]{:S(2)}, u32[]{:S(2)}) async-start(bf16[8,4,16,256]{3,2,1,0:T(8,128)(2,1)} %broadcast_select_fusion), calls=%async_computation.1 | async-start | bytes 524288 | tf_op jit(solution)/shard_map/all_to_all | solution.py:210
  45.7 13.9 %collective-permute-start.4 = (bf16[256,1024]{1,0:T(8,128)(2,1)S(1)}, bf16[256,1024]{1,0:T(8,128)(2,1)S(1)}, u32[]{:S(2)}, u32[]{:S(2)}) collective-permute-start(bf16[256,1024]{1,0:T(8,128)(2,1)S(1)} %collective-permute-done.2), channel_id=1, source_target_pairs={{0,112},{8,120},{16,0},{24,8},{32,16},{40,24},{48,32},{56,40},{64,... | collective-permute-start | bytes 1572872 | tf_op jit(solution)/shard_map/ppermute | solution.py:34
  50.9 15.1 %collective-permute-start.5 = (bf16[256,1024]{1,0:T(8,128)(2,1)}, bf16[256,1024]{1,0:T(8,128)(2,1)S(1)}, u32[]{:S(2)}, u32[]{:S(2)}) collective-permute-start(bf16[256,1024]{1,0:T(8,128)(2,1)} %collective-permute-done.3), channel_id=1, source_target_pairs={{0,16},{8,24},{16,32},{24,40},{32,48},{40,56},{48,64},{56,72},{64,... | collective-permute-start | bytes 1572872 | tf_op jit(solution)/shard_map/ppermute | solution.py:34
  59.6 13.0 %collective-permute-start.6 = (bf16[256,1024]{1,0:T(8,128)(2,1)S(1)}, bf16[256,1024]{1,0:T(8,128)(2,1)S(1)}, u32[]{:S(2)}, u32[]{:S(2)}) collective-permute-start(bf16[256,1024]{1,0:T(8,128)(2,1)S(1)} %collective-permute-done.4), channel_id=1, source_target_pairs={{0,112},{8,120},{16,0},{24,8},{32,16},{40,24},{48,32},{56,40},{64,... | collective-permute-start | bytes 1572872 | tf_op jit(solution)/shard_map/ppermute | solution.py:34
  66.0 11.1 %collective-permute-start.7 = (bf16[128,1024]{1,0:T(8,128)(2,1)S(1)}, bf16[128,1024]{1,0:T(8,128)(2,1)S(1)}, u32[]{:S(2)}, u32[]{:S(2)}) collective-permute-start(bf16[128,1024]{1,0:T(8,128)(2,1)S(1)} %slice.82), channel_id=1, source_target_pairs={{0,16},{8,24},{16,32},{24,40},{32,48},{40,56},{48,64},{56,72},{64,... | collective-permute-start | bytes 786440 | tf_op jit(solution)/shard_map/ppermute | solution.py:34
  72.6 7.4 %collective-permute-start.8 = (bf16[128,1024]{1,0:T(8,128)(2,1)S(1)}, bf16[128,1024]{1,0:T(8,128)(2,1)S(1)}, u32[]{:S(2)}, u32[]{:S(2)}) collective-permute-start(bf16[128,1024]{1,0:T(8,128)(2,1)S(1)} %slice.83), channel_id=1, source_target_pairs={{0,112},{8,120},{16,0},{24,8},{32,16},{40,24},{48,32},{56,40},{64,... | collective-permute-start | bytes 786440 | tf_op jit(solution)/shard_map/ppermute | solution.py:34
  80.9 7.1 %collective-permute-start.10 = (bf16[128,1024]{1,0:T(8,128)(2,1)S(1)}, bf16[128,1024]{1,0:T(8,128)(2,1)S(1)}, u32[]{:S(2)}, u32[]{:S(2)}) collective-permute-start(bf16[128,1024]{1,0:T(8,128)(2,1)S(1)} %get-tuple-element.37), channel_id=1, source_target_pairs={{0,1},{1,2},{2,3},{3,4},{4,5},{5,6},{6,7},{7,0},{8,9},{9,10},{10,1... | collective-permute-start | bytes 786440 | tf_op jit(solution)/shard_map/ppermute | solution.py:42
  85.4 8.4 %collective-permute-start.13 = (bf16[128,1024]{1,0:T(8,128)(2,1)S(1)}, bf16[128,1024]{1,0:T(8,128)(2,1)S(1)}, u32[]{:S(2)}, u32[]{:S(2)}) collective-permute-start(bf16[128,1024]{1,0:T(8,128)(2,1)S(1)} %get-tuple-element.36), channel_id=1, source_target_pairs={{0,7},{1,0},{2,1},{3,2},{4,3},{5,4},{6,5},{7,6},{8,15},{9,8},{10,9... | collective-permute-start | bytes 786440 | tf_op jit(solution)/shard_map/ppermute | solution.py:42
  86.1 7.8 %collective-permute-start.14 = (bf16[128,1024]{1,0:T(8,128)(2,1)S(1)}, bf16[128,1024]{1,0:T(8,128)(2,1)S(1)}, u32[]{:S(2)}, u32[]{:S(2)}) collective-permute-start(bf16[128,1024]{1,0:T(8,128)(2,1)S(1)} %get-tuple-element.35), channel_id=1, source_target_pairs={{0,1},{1,2},{2,3},{3,4},{4,5},{5,6},{6,7},{7,0},{8,9},{9,10},{10,1... | collective-permute-start | bytes 786440 | tf_op jit(solution)/shard_map/ppermute | solution.py:42
  88.2 11.3 %collective-permute-start.11 = (bf16[128,1024]{1,0:T(8,128)(2,1)S(1)}, bf16[128,1024]{1,0:T(8,128)(2,1)S(1)}, u32[]{:S(2)}, u32[]{:S(2)}) collective-permute-start(bf16[128,1024]{1,0:T(8,128)(2,1)S(1)} %get-tuple-element.40), channel_id=1, source_target_pairs={{0,7},{1,0},{2,1},{3,2},{4,3},{5,4},{6,5},{7,6},{8,15},{9,8},{10,9... | collective-permute-start | bytes 786440 | tf_op jit(solution)/shard_map/ppermute | solution.py:42
  90.4 9.0 %collective-permute-start.12 = (bf16[128,1024]{1,0:T(8,128)(2,1)S(1)}, bf16[128,1024]{1,0:T(8,128)(2,1)S(1)}, u32[]{:S(2)}, u32[]{:S(2)}) collective-permute-start(bf16[128,1024]{1,0:T(8,128)(2,1)S(1)} %get-tuple-element.39), channel_id=1, source_target_pairs={{0,1},{1,2},{2,3},{3,4},{4,5},{5,6},{6,7},{7,0},{8,9},{9,10},{10,1... | collective-permute-start | bytes 786440 | tf_op jit(solution)/shard_map/ppermute | solution.py:42
  100.7 28.4 %collective-permute-start.15 = (bf16[256,1024]{1,0:T(8,128)(2,1)}, bf16[256,1024]{1,0:T(8,128)(2,1)S(1)}, u32[]{:S(2)}, u32[]{:S(2)}) collective-permute-start(bf16[256,1024]{1,0:T(8,128)(2,1)} %get-tuple-element.34), channel_id=1, source_target_pairs={{0,7},{1,0},{2,1},{3,2},{4,3},{5,4},{6,5},{7,6},{8,15},{9,8},{10,9... | collective-permute-start | bytes 1572872 | tf_op jit(solution)/shard_map/ppermute | solution.py:42
  102.8 26.2 %collective-permute-start.16 = (bf16[256,1024]{1,0:T(8,128)(2,1)S(1)}, bf16[256,1024]{1,0:T(8,128)(2,1)}, u32[]{:S(2)}, u32[]{:S(2)}) collective-permute-start(bf16[256,1024]{1,0:T(8,128)(2,1)S(1)} %get-tuple-element.33), channel_id=1, source_target_pairs={{0,1},{1,2},{2,3},{3,4},{4,5},{5,6},{6,7},{7,0},{8,9},{9,10},{10,1... | collective-permute-start | bytes 1572872 | tf_op jit(solution)/shard_map/ppermute | solution.py:42
  117.7 20.8 %all-to-all-start.3 = ((bf16[16,16,256]{2,1,0:T(8,128)(2,1)}), bf16[16,16,256]{2,1,0:T(8,128)(2,1)S(1)}, u32[]{:S(2)}, u32[]{:S(2)}) async-start(bf16[16,16,256]{2,1,0:T(8,128)(2,1)} %broadcast_in_dim.125), calls=%async_computation.3 | async-start | bytes 262144 | tf_op jit(solution)/shard_map/all_to_all | solution.py:257
  131.7 7.8 %collective-permute-start.17 = (bf16[256,512]{1,0:T(8,128)(2,1)}, bf16[256,512]{1,0:T(8,128)(2,1)S(1)}, u32[]{:S(2)}, u32[]{:S(2)}) collective-permute-start(bf16[256,512]{1,0:T(8,128)(2,1)} %get-tuple-element.41), channel_id=1, source_target_pairs={{0,7},{1,0},{2,1},{3,2},{4,3},{5,4},{6,5},{7,6},{8,15},{9,8},{10,9... | collective-permute-start | bytes 786440 | tf_op jit(solution)/shard_map/ppermute | solution.py:42
  132.7 8.7 %collective-permute-start.18 = (bf16[256,512]{1,0:T(8,128)(2,1)}, bf16[256,512]{1,0:T(8,128)(2,1)S(1)}, u32[]{:S(2)}, u32[]{:S(2)}) collective-permute-start(bf16[256,512]{1,0:T(8,128)(2,1)} %get-tuple-element.43), channel_id=1, source_target_pairs={{0,1},{1,2},{2,3},{3,4},{4,5},{5,6},{6,7},{7,0},{8,9},{9,10},{10,1... | collective-permute-start | bytes 786440 | tf_op jit(solution)/shard_map/ppermute | solution.py:42
  136.6 9.2 %collective-permute-start.20 = (bf16[256,512]{1,0:T(8,128)(2,1)}, bf16[256,512]{1,0:T(8,128)(2,1)S(1)}, u32[]{:S(2)}, u32[]{:S(2)}) collective-permute-start(bf16[256,512]{1,0:T(8,128)(2,1)} %get-tuple-element.42), channel_id=1, source_target_pairs={{0,15},{1,8},{2,9},{3,10},{4,11},{5,12},{6,13},{7,14},{8,7},{9,0},... | collective-permute-start | bytes 786440 | tf_op jit(solution)/shard_map/ppermute | solution.py:51
  137.9 10.0 %collective-permute-start.21 = (bf16[256,512]{1,0:T(8,128)(2,1)}, bf16[256,512]{1,0:T(8,128)(2,1)S(1)}, u32[]{:S(2)}, u32[]{:S(2)}) collective-permute-start(bf16[256,512]{1,0:T(8,128)(2,1)} %get-tuple-element.44), channel_id=1, source_target_pairs={{0,9},{1,10},{2,11},{3,12},{4,13},{5,14},{6,15},{7,8},{8,1},{9,2},... | collective-permute-start | bytes 786440 | tf_op jit(solution)/shard_map/ppermute | solution.py:51
  (7 other events, 74.4 us)
